TPU v7x, 128 devices: a whole 4x4x4 slice. The times are simulated.
128 devices in a mesh: lat: 32 (over z, y, x_hi), lev: 4 (over x_lo, core).
Axes of the slice: x: 4 (x_hi: 2, x_lo: 2; x = x_hi * 2 + x_lo), y: 4, z: 4, core: 2. Of those that a mesh axis runs over, the one named last changes fastest.
Arguments:
- spec_in: bfloat16 [192, 171, 4, 512], P('lat', None, None, 'lev'), may hold values from -6 to 6
- cotangent: bfloat16 [192, 171, 4, 512], P('lat', None, None, 'lev'), may hold values from -6 to 6
- legendre: bfloat16 [192, 171, 256], P('lat'), may hold values from -0.4375 to 0.4375
- quad_weights: float32 [256], replicated, may hold values from 0.5 to 2
- wave_order: int32 [192], replicated, may hold values from 0 to 191, each once
- norm_gain: float32 [256], replicated, may hold values from 0.5 to 1.5
- weight_in: bfloat16 [256, 512], replicated, may hold values from -0.375 to 0.375
- bias_in: float32 [512], replicated, may hold values from -3 to 3
- weight_mid: bfloat16 [512, 512], replicated, may hold values from -0.25 to 0.25
- bias_mid: float32 [512], replicated, may hold values from -3 to 3
- weight_out: bfloat16 [512, 256], replicated, may hold values from -0.25 to 0.25
Outputs:
- grad_spec: float32 [192, 171, 4, 512], P('lat', None, None, 'lev')
- grad_gain: float32 [256], replicated
- grad_w_in: float32 [256, 512], replicated
- grad_b_in: float32 [512], replicated
- grad_w_mid: float32 [512, 512], replicated
- grad_b_mid: float32 [512], replicated
- grad_w_out: float32 [512, 256], replicated
Inputs may be any that keep to these rules, and one draw needn't show every extreme that they name: `wave_order`: each of 0 to 191 appears once; a slot holding 171 or more is unused.
All inputs are finite; a program needn't handle non-finite values.
Results may differ from a plain program's by a relative error of at most 0.007.
Values may be sent and summed in bfloat16 or wider, within the bound.
A program may use at most 128 MiB of HBM per device.

v0:
```python
import math

import jax
import jax.numpy as jnp
from jax import lax
from jax.sharding import PartitionSpec as P

WAVES = 171
NLAT = 256
NLON = 512
MEMBERS = 4


time_step = 0.5
norm_eps = 1e-06


def in_one_piece(arrays, axis, split_dim, concat_dim, along):
    ends, at = ([], 0)
    for a in arrays[:-1]:
        at += a.shape[along]
        ends.append(at)
    both = jnp.concatenate(arrays, axis=along)
    return tuple(
        jnp.split(
            lax.all_to_all(both, axis, split_axis=split_dim, concat_axis=concat_dim, tiled=True),
            ends,
            axis=along,
        )
    )


def spectral_masks(waves_held, degree_count):
    degree = jnp.arange(degree_count, dtype=jnp.int32)
    living = (waves_held[:, None] <= degree[None, :]) & (waves_held[:, None] < WAVES)
    ratio = (degree * (degree + 1)).astype(jnp.float32) / float(WAVES * (WAVES - 1))
    factor = 1.0 / (1.0 + ratio * ratio)
    shrink = jnp.where(living, factor[None, :], jnp.zeros_like(factor)[None, :])
    return (living, shrink)


def fourier_table(waves_all):
    longitude = jnp.arange(NLON, dtype=jnp.int32)
    phase_steps = waves_all[:, None] * longitude[None, :] % NLON
    angles = phase_steps.astype(jnp.float32) * (2.0 * math.pi / NLON)
    weight_scale = jnp.where(waves_all < WAVES, math.sqrt(2.0 / NLON), 0.0).astype(jnp.float32)[
        :, None
    ]
    return jnp.stack(
        [jnp.cos(angles) * weight_scale, -jnp.sin(angles) * weight_scale], axis=1
    ).astype(jnp.bfloat16)


def contract_rows(left, right):
    return lax.dot_general(
        left, right, (((0,), (0,)), ((), ())), preferred_element_type=jnp.float32
    )


def contract_cols(left, right):
    return lax.dot_general(
        left, right, (((1,), (1,)), ((), ())), preferred_element_type=jnp.float32
    )


def column_grads(
    columns, column_cot, norm_gain, weight_in, bias_in, weight_mid, bias_mid, weight_out
):
    inputs = columns.astype(jnp.float32)
    inverse = lax.rsqrt(jnp.mean(inputs * inputs, axis=1, keepdims=True) + norm_eps)
    normed = (inputs * inverse * norm_gain).astype(jnp.bfloat16)
    pre_one = jnp.dot(normed, weight_in, preferred_element_type=jnp.float32) + bias_in
    sig_one = jax.nn.sigmoid(pre_one)
    act_one = (pre_one * sig_one).astype(jnp.bfloat16)
    pre_two = jnp.dot(act_one, weight_mid, preferred_element_type=jnp.float32) + bias_mid
    sig_two = jax.nn.sigmoid(pre_two)
    act_two = (pre_two * sig_two).astype(jnp.bfloat16)
    gradient_third = contract_rows(act_two, column_cot)
    back_two = contract_cols(column_cot, weight_out)
    delta_two = (back_two * sig_two * (1.0 + pre_two * (1.0 - sig_two))).astype(jnp.bfloat16)
    gradient_second = contract_rows(act_one, delta_two)
    offset_second = jnp.sum(delta_two.astype(jnp.float32), axis=0)
    back_one = contract_cols(delta_two, weight_mid)
    delta_one = (back_one * sig_one * (1.0 + pre_one * (1.0 - sig_one))).astype(jnp.bfloat16)
    gradient_first = contract_rows(normed, delta_one)
    offset_first = jnp.sum(delta_one.astype(jnp.float32), axis=0)
    back_norm = contract_cols(delta_one, weight_in)
    gradient_gain = jnp.sum(back_norm * inputs * inverse, axis=0)
    scaled = back_norm * norm_gain
    grad_columns = inverse * scaled - inputs * inverse * inverse * inverse * jnp.mean(
        scaled * inputs, axis=1, keepdims=True
    )
    return (
        grad_columns.astype(jnp.bfloat16),
        (
            gradient_gain,
            gradient_first,
            offset_first,
            gradient_second,
            offset_second,
            gradient_third,
        ),
    )


def synthesize(wave_table, coeffs):
    shape = coeffs.shape
    split = coeffs.reshape(shape[0], shape[1], shape[2], shape[3] // 2, 2)
    return jnp.einsum(
        "spo,stecp->otec", wave_table, split, preferred_element_type=jnp.float32
    ).astype(jnp.bfloat16)


def analyze(wave_table, values):
    result = jnp.einsum(
        "spo,otec->stecp", wave_table, values, preferred_element_type=jnp.float32
    ).astype(jnp.bfloat16)
    shape = result.shape
    return result.reshape(shape[0], shape[1], shape[2], shape[3] * 2)


def local(
    spec_in,
    cotangent,
    legendre,
    quad_weights,
    wave_order,
    norm_gain,
    weight_in,
    bias_in,
    weight_mid,
    bias_mid,
    weight_out,
):
    slots_here = spec_in.shape[0]
    own_waves = lax.dynamic_slice_in_dim(wave_order, lax.axis_index("lat") * slots_here, slots_here)
    living, shrink = spectral_masks(own_waves, spec_in.shape[1])
    basis_rows = jnp.where(living[:, :, None], legendre, jnp.zeros_like(legendre))
    wave_table = fourier_table(wave_order)
    fourier = jnp.einsum(
        "slt,slek->stek", basis_rows, spec_in, preferred_element_type=jnp.float32
    ).astype(jnp.bfloat16)
    pushed = (time_step * cotangent.astype(jnp.float32) * shrink[:, :, None, None]).astype(
        jnp.bfloat16
    )
    pulled = jnp.einsum("slt,slek->stek", basis_rows, pushed, preferred_element_type=jnp.float32)
    pulled = (quad_weights[None, :, None, None] * pulled).astype(jnp.bfloat16)
    fourier_all, pulled_all = in_one_piece((fourier, pulled), "lat", 1, 0, 2)
    grid_part = synthesize(wave_table, fourier_all)
    cot_part = synthesize(wave_table, pulled_all)
    grid_values, grid_cot = in_one_piece((grid_part, cot_part), "lev", 0, 3, 1)
    grid_shape = grid_values.shape
    grad_rows, grads_local = column_grads(
        grid_values.reshape(-1, grid_shape[3]),
        grid_cot.reshape(-1, grid_shape[3]),
        norm_gain,
        weight_in,
        bias_in,
        weight_mid,
        bias_mid,
        weight_out,
    )
    grad_grid = grad_rows.reshape(grid_shape)
    grad_part = lax.all_to_all(grad_grid, "lev", split_axis=3, concat_axis=0, tiled=True)
    back_fourier = analyze(wave_table, grad_part)
    back_slots = lax.all_to_all(back_fourier, "lat", split_axis=0, concat_axis=1, tiled=True)
    summed = lax.psum(
        (
            grads_local[0],
            grads_local[1],
            grads_local[2],
            grads_local[3],
            grads_local[4],
            grads_local[5],
        ),
        ("lat", "lev"),
    )
    factor = float(MEMBERS * NLAT * NLON) ** (-0.5)
    grads = tuple((piece * factor for piece in summed))
    grad_spec = cotangent.astype(jnp.float32) * shrink[:, :, None, None] + jnp.einsum(
        "slt,stek->slek", basis_rows, back_slots, preferred_element_type=jnp.float32
    )
    return (grad_spec, grads[0], grads[1], grads[2], grads[3], grads[4], grads[5])


def solution(mesh):
    placed = (
        P("lat", None, None, "lev"),
        P("lat", None, None, "lev"),
        P("lat", None, None),
        P(),
        P(),
        P(),
        P(),
        P(),
        P(),
        P(),
        P(),
    )
    return jax.shard_map(
        local,
        mesh=mesh,
        in_specs=placed,
        out_specs=(P("lat", None, None, "lev"), P(), P(), P(), P(), P(), P()),
        check_vma=False,
    )
```

profile of v0, /device:TPU:1, one launch (start us, length us, event | category | flops | bytes accessed | tf_op | source)
XLA Modules:
  0.0 443.0 jit_solution(5164331908292639618)
XLA Ops:
  17.2 11.8 %all-to-all-start = ((bf16[6,256,8,128]{3,2,0,1:T(8,128)(2,1)}), bf16[6,256,8,128]{3,2,0,1:T(8,128)(2,1)}, u32[]{:S(2)}, u32[]{:S(2)}) async-start(bf16[6,256,8,128]{3,2,0,1:T(8,128)(2,1)} %copy.95), calls=%async_computation | async-start | bytes 6291456 | tf_op jit(solution)/shard_map/all_to_all | solution.py:26
  30.9 38.7 %all-to-all-done = bf16[6,256,8,128]{3,2,0,1:T(8,128)(2,1)} async-done(((bf16[6,256,8,128]{3,2,0,1:T(8,128)(2,1)}), bf16[6,256,8,128]{3,2,0,1:T(8,128)(2,1)}, u32[]{:S(2)}, u32[]{:S(2)}) %all-to-all-start) | async-done | bytes 3145760 | tf_op jit(solution)/shard_map/all_to_all | solution.py:26
  74.5 5.3 %copy.98 = bf16[192,8,4,128]{0,1,3,2:T(8,128)(2,1)} copy(bf16[192,8,4,128]{3,2,1,0:T(4,128)(2,1)} %get-tuple-element.61) | data formatting | bytes 3145728 | tf_op jit(solution)/shard_map/split | solution.py:25
  79.9 4.2 copy.100
  84.1 3.7 bitcast_convert_fusion.1
  92.2 13.8 %copy.102 = bf16[512,16,4,64]{3,2,1,0:T(4,128)(2,1)} copy(bf16[512,16,4,64]{0,3,2,1:T(8,128)(2,1)} %pad_maximum_fusion) | data formatting | bytes 8388608 | tf_op jit(solution)/shard_map/concatenate | solution.py:23
  106.0 9.5 %reshape.301 = bf16[4,2,262144]{2,1,0:T(2,128)(2,1)} reshape(bf16[512,16,4,64]{3,2,1,0:T(4,128)(2,1)} %copy.102) | data formatting | bytes 8388608
  115.6 55.2 %all_to_all.72 = bf16[4,2,262144]{2,1,0:T(2,128)(2,1)} all-to-all(bf16[4,2,262144]{2,1,0:T(2,128)(2,1)} %reshape.301), channel_id=1, replica_groups=mesh['lat'=32,'lev'=4] {'lev'}, dimensions={0} | all-to-all | bytes 8388608 | tf_op jit(solution)/shard_map/all_to_all | solution.py:26
  170.7 9.3 %reshape.302 = bf16[512,16,4,64]{3,2,1,0:T(4,128)(2,1)} reshape(bf16[4,2,262144]{2,1,0:T(2,128)(2,1)} %all_to_all.72) | data formatting | bytes 8388608
  180.0 12.7 %copy.104 = bf16[128,16,4,4,64]{0,4,3,2,1:T(8,128)(2,1)} copy(bf16[128,16,4,4,64]{4,2,1,0,3:T(4,128)(2,1)} %bitcast.65) | data formatting | bytes 8388608 | tf_op jit(solution)/shard_map/all_to_all | solution.py:26
  194.8 4.7 %fusion.44 = (bf16[128,8,4,256]{0,3,2,1:T(8,128)(2,1)S(1)}, f32[128,8,4,256]{0,3,2,1:T(8,128)}) fusion(bf16[128,16,4,256]{0,3,2,1:T(8,128)(2,1)} %bitcast.67), kind=kLoop, calls=%fused_computation.85 | loop fusion | flops 1048576 | bytes 10485760 | tf_op jit(solution)/shard_map/split | solution.py:25
  205.5 6.3 %copy.108 = f32[128,8,4,256]{3,2,1,0:T(4,128)} copy(f32[128,8,4,256]{0,3,2,1:T(8,128)} %get-tuple-element.60) | data formatting | bytes 8388608 | tf_op jit(solution)/shard_map/convert_element_type | solution.py:69
  211.8 5.4 %reshape.294 = f32[4096,256]{1,0:T(8,128)} reshape(f32[128,8,4,256]{3,2,1,0:T(4,128)} %copy.108) | data formatting | bytes 8388608 | tf_op jit(solution)/shard_map/convert_element_type | solution.py:69
  217.2 4.9 %multiply_convert_fusion.3 = (bf16[4096,512]{1,0:T(8,128)(2,1)S(1)}, f32[4096,512]{1,0:T(8,128)S(1)}) fusion(f32[512]{0:T(512)S(1)} %copy-done.17, bf16[256,512]{1,0:T(8,128)(2,1)S(1)} %copy-done.10, f32[4096,256]{1,0:T(8,128)} %reshape.294, f32[256]{0:T(256)S(1)} %copy-done.14, f32[4096]{0:T(1024)S(1)} %rsqrt.12), kind=kOutput, calls=%fused_computation.6 | convolution fusion | flops 1089470464 | bytes 17058816 | tf_op jit(solution)/shard_map/dot_general | solution.py:72
  224.6 3.9 convert_reduce_fusion
  231.8 4.7 %convert_reduce_fusion.1 = (f32[512]{0:T(512)S(1)}, bf16[4096,512]{1,0:T(8,128)(2,1)S(1)}) fusion(f32[4096,512]{1,0:T(8,128)S(1)} %get-tuple-element.68, f32[512]{0:T(512)S(1)} %copy-done.17, bf16[4096,512]{1,0:T(8,128)(2,1)S(1)} %get-tuple-element.73, bf16[512,512]{1,0:T(8,128)(2,1)S(1)} %copy-done.9), kind=kOutput, calls=%fused_computation.2 | convolution fusion | flops 2172648960 | bytes 17305600 | tf_op jit(solution)/shard_map/dot_general | solution.py:61
  244.2 4.1 copy.109
  248.3 4.6 %all-to-all-start.2 = ((bf16[128,8,4,256]{0,2,1,3:T(4,128)(2,1)}), bf16[128,8,4,256]{0,2,1,3:T(4,128)(2,1)S(1)}, u32[]{:S(2)}, u32[]{:S(2)}) async-start(bf16[128,8,4,256]{0,2,1,3:T(4,128)(2,1)} %copy.109), calls=%async_computation.2 | async-start | bytes 4194304 | tf_op jit(solution)/shard_map/all_to_all | solution.py:164
  252.9 6.9 %fusion.42 = f32[256,512]{1,0:T(8,128)} fusion(bf16[4096,512]{1,0:T(8,128)(2,1)} %copy-done.3, f32[4096,256]{1,0:T(8,128)} %reshape.294, f32[256]{0:T(256)S(1)} %copy-done.14, f32[4096]{0:T(1024)S(1)} %rsqrt.12), kind=kOutput, calls=%fused_computation.83 | convolution fusion | flops 1076887552 | bytes 8930304 | tf_op jit(solution)/shard_map/dot_general | solution.py:55
  259.8 6.6 %fusion = f32[512,256]{1,0:T(8,128)} fusion(bf16[4096,256]{1,0:T(8,128)(2,1)S(1)} %copy-done.8, f32[4096,512]{1,0:T(8,128)} %copy-done.4, f32[512]{0:T(512)S(1)} %copy-done.18), kind=kOutput, calls=%fused_computation.16 | convolution fusion | flops 1086324736 | bytes 11012096 | tf_op jit(solution)/shard_map/dot_general | solution.py:55
  266.5 11.4 %all-to-all-done.2 = bf16[128,8,4,256]{0,2,1,3:T(4,128)(2,1)S(1)} async-done(((bf16[128,8,4,256]{0,2,1,3:T(4,128)(2,1)}), bf16[128,8,4,256]{0,2,1,3:T(4,128)(2,1)S(1)}, u32[]{:S(2)}, u32[]{:S(2)}) %all-to-all-start.2) | async-done | bytes 2097184 | tf_op jit(solution)/shard_map/all_to_all | solution.py:164
  290.4 8.1 %all-to-all-start.3 = ((bf16[192,8,4,128]{3,1,2,0:T(8,128)(2,1)}), bf16[192,8,4,128]{3,1,2,0:T(8,128)(2,1)S(1)}, u32[]{:S(2)}, u32[]{:S(2)}) async-start(bf16[192,8,4,128]{3,1,2,0:T(8,128)(2,1)} %copy.113), calls=%async_computation.3 | async-start | bytes 3145728 | tf_op jit(solution)/shard_map/all_to_all | solution.py:166
  298.5 76.7 %all-reduce = (f32[256]{0:T(256)S(1)}, f32[512]{0:T(512)S(1)}, f32[512]{0:T(512)S(1)}) all-reduce(f32[256]{0:T(256)S(1)} %get-tuple-element.49, f32[512]{0:T(512)S(1)} %get-tuple-element.70, f32[512]{0:T(512)S(1)} %get-tuple-element.72), channel_id=1, replica_groups=mesh['lat'=32,'lev'=4] {'lat','lev'}, use_global_device_ids=true, to_apply=%region_3.4 | all-reduce | flops 1280 | bytes 10240 | tf_op jit(solution)/shard_map/psum | solution.py:167
  376.3 49.5 %all-reduce.4.cloned.1.call-done = (f32[256,512]{1,0:T(8,128)}, f32[512,512]{1,0:T(8,128)}, f32[512,256]{1,0:T(8,128)}) async-done(((f32[256,512]{1,0:T(8,128)}, f32[512,512]{1,0:T(8,128)}, f32[512,256]{1,0:T(8,128)}), (f32[256,512]{1,0:T(8,128)}, f32[512,512]{1,0:T(8,128)}, f32[512,256]{1,0:T(8,128)})) %all-reduce.4.cloned.1.call-update) | async-done | bytes 2097168 | tf_op jit(solution)/shard_map/psum | solution.py:167
  (80 shorter events, 66.4 us)
Async XLA Ops:
  7.2 1.6 copy-start
  8.1 2.6 copy-start.12
  17.2 11.8 %copy-start.15 = (s32[192]{0:T(256)S(1)}, s32[192]{0:T(256)}, u32[]{:S(2)}) copy-start(s32[192]{0:T(256)} %param.15) | copy-start | bytes 2308
  17.2 52.4 %all-to-all-start = ((bf16[6,256,8,128]{3,2,0,1:T(8,128)(2,1)}), bf16[6,256,8,128]{3,2,0,1:T(8,128)(2,1)}, u32[]{:S(2)}, u32[]{:S(2)}) async-start(bf16[6,256,8,128]{3,2,0,1:T(8,128)(2,1)} %copy.95), calls=%async_computation | async-start | bytes 6291456 | tf_op jit(solution)/shard_map/all_to_all | solution.py:26
  84.1 3.7 copy-start.6
  205.5 19.1 %copy-start.7 = (bf16[4096,256]{1,0:T(8,128)(2,1)}, bf16[4096,256]{1,0:T(8,128)(2,1)S(1)}, u32[]{:S(2)}) copy-start(bf16[4096,256]{1,0:T(8,128)(2,1)S(1)} %reshape.291) | copy-start | bytes 6291460
  211.8 5.4 %copy-start.10 = (bf16[256,512]{1,0:T(8,128)(2,1)S(1)}, bf16[256,512]{1,0:T(8,128)(2,1)}, u32[]{:S(2)}) copy-start(bf16[256,512]{1,0:T(8,128)(2,1)} %param.17) | copy-start | bytes 786436
  211.8 5.4 %copy-start.14 = (f32[256]{0:T(256)S(1)}, f32[256]{0:T(256)}, u32[]{:S(2)}) copy-start(f32[256]{0:T(256)} %param.16) | copy-start | bytes 3076
  211.8 5.4 %copy-start.17 = (f32[512]{0:T(512)S(1)}, f32[512]{0:T(512)}, u32[]{:S(2)}) copy-start(f32[512]{0:T(512)} %param.18) | copy-start | bytes 6148
  217.2 4.9 %copy-start.9 = (bf16[512,512]{1,0:T(8,128)(2,1)S(1)}, bf16[512,512]{1,0:T(8,128)(2,1)}, u32[]{:S(2)}) copy-start(bf16[512,512]{1,0:T(8,128)(2,1)} %param.19) | copy-start | bytes 1572868
  222.1 2.5 copy-start.16
  222.1 2.5 copy-start.18
  224.6 3.9 copy-start.4
  231.8 4.7 %copy-start.2 = (f32[4096,256]{1,0:T(8,128)S(1)}, f32[4096,256]{1,0:T(8,128)}, u32[]{:S(2)}) copy-start(f32[4096,256]{1,0:T(8,128)} %reshape.294) | copy-start | bytes 12582916
  236.5 1.9 copy-start.3
  248.3 29.6 %all-to-all-start.2 = ((bf16[128,8,4,256]{0,2,1,3:T(4,128)(2,1)}), bf16[128,8,4,256]{0,2,1,3:T(4,128)(2,1)S(1)}, u32[]{:S(2)}, u32[]{:S(2)}) async-start(bf16[128,8,4,256]{0,2,1,3:T(4,128)(2,1)} %copy.109), calls=%async_computation.2 | async-start | bytes 4194304 | tf_op jit(solution)/shard_map/all_to_all | solution.py:164
  252.9 172.9 %all-reduce.4.cloned.1.call-start = ((), (), s32[]{:S(2)}) async-start(), calls=%async_computation.4 | async-start | bytes 4194304 | tf_op jit(solution)/shard_map/psum | solution.py:167
  252.9 6.9 %copy-start.8 = (bf16[4096,256]{1,0:T(8,128)(2,1)S(1)}, bf16[4096,256]{1,0:T(8,128)(2,1)}, u32[]{:S(2)}) copy-start(bf16[4096,256]{1,0:T(8,128)(2,1)} %copy-done.7) | copy-start | bytes 6291460
  290.4 141.5 %copy-start.5 = (bf16[6,171,256]{2,1,0:T(8,128)(2,1)S(1)}, bf16[6,171,256]{2,1,0:T(8,128)(2,1)}, u32[]{:S(2)}) copy-start(bf16[6,171,256]{2,1,0:T(8,128)(2,1)} %param.13) | copy-start | bytes 1575940
  290.4 141.5 %copy-start.11 = (f32[6,171]{1,0:T(8,128)S(1)}, f32[6,171]{1,0:T(8,128)}, u32[]{:S(2)}) copy-start(f32[6,171]{1,0:T(8,128)} %get-tuple-element.63) | copy-start | bytes 12316
  290.4 141.5 %copy-start.13 = (pred[6,171]{1,0:T(8,128)(4,1)S(1)}, pred[6,171]{1,0:T(8,128)(4,1)}, u32[]{:S(2)}) copy-start(pred[6,171]{1,0:T(8,128)(4,1)} %copy-done.12) | copy-start | bytes 3082
  290.4 141.5 %all-to-all-start.3 = ((bf16[192,8,4,128]{3,1,2,0:T(8,128)(2,1)}), bf16[192,8,4,128]{3,1,2,0:T(8,128)(2,1)S(1)}, u32[]{:S(2)}, u32[]{:S(2)}) async-start(bf16[192,8,4,128]{3,1,2,0:T(8,128)(2,1)} %copy.113), calls=%async_computation.3 | async-start | bytes 3145728 | tf_op jit(solution)/shard_map/all_to_all | solution.py:166
  431.8 4.1 copy-start.1
Sparse Core Ops, SparseCore 0:
  266.6 159.1 all-reduce.3
where the time goes:
time: 449 us; the launch traced here: 443 us
  blocking collectives  132 us (29%)
  local copies, waits for them, and re-layouts  99.6 us (22%)
  waiting for transfers between devices  99.6 us (22%)
  matrix products  49.6 us (11%)
  starting transfers between devices  24.5 us (5%)
  other arithmetic  23.3 us (5%)
  between operations  14.5 us (3%)
    psum x1, blocking collectives, local(): lax.psum((grads_local[0], grads_local[1], grads_local[2], grads_local[3],...  76.7 us
    all_to_all x1, blocking collectives, in_one_piece(): lax.all_to_all(both, axis, split_axis=split_dim, concat_axis=concat_dim,...  55.2 us
    psum x1, waiting for transfers between devices, local(): lax.psum((grads_local[0], grads_local[1], grads_local[2], grads_local[3],...  49.5 us
    all_to_all x1, waiting for transfers between devices, in_one_piece(): lax.all_to_all(both, axis, split_axis=split_dim, concat_axis=concat_dim,...  38.7 us
    unnamed x41, local copies, waits for them, and re-layouts  21.1 us
    concatenate x2, local copies, waits for them, and re-layouts, in_one_piece(): both = jnp.concatenate(arrays, axis=along)  17.5 us
    dot_general x3, matrix products, contract_rows(): lax.dot_general(left, right, (((0,), (0,)), ((), ())), preferred_element_...  16.9 us
    all_to_all x2, local copies, waits for them, and re-layouts, in_one_piece(): lax.all_to_all(both, axis, split_axis=split_dim, concat_axis=concat_dim,...  15.5 us
  transfers between devices with their start and end apart: 4, of which 3 were waited for; matrix products, arithmetic and copies ran while one was open for 8% of the time, Pallas kernels for 0%

commit v1 on v0

v1 whole, which is shorter than its diff:
```python
import functools
import math

import jax
import jax.numpy as jnp
import numpy as np
from jax import lax
from jax.experimental import pallas as pl
from jax.experimental.pallas import tpu as pltpu
from jax.sharding import PartitionSpec as P

WAVES = 171
NLAT = 256
NLON = 512
MEMBERS = 4

time_step = 0.5
norm_eps = 1e-06
MESH = pl.DeviceIdType.MESH


def spectral_masks(waves_held, degree_count):
    degree = jnp.arange(degree_count, dtype=jnp.int32)
    living = (waves_held[:, None] <= degree[None, :]) & (waves_held[:, None] < WAVES)
    ratio = (degree * (degree + 1)).astype(jnp.float32) / float(WAVES * (WAVES - 1))
    factor = 1.0 / (1.0 + ratio * ratio)
    shrink = jnp.where(living, factor[None, :], jnp.zeros_like(factor)[None, :])
    return (living, shrink)


def fourier_tables(waves_all):
    longitude = jnp.arange(NLON, dtype=jnp.int32)
    phase_steps = waves_all[:, None] * longitude[None, :] % NLON
    angles = phase_steps.astype(jnp.float32) * (2.0 * math.pi / NLON)
    weight_scale = jnp.where(waves_all < WAVES, math.sqrt(2.0 / NLON), 0.0).astype(jnp.float32)[
        :, None
    ]
    table = jnp.concatenate(
        [jnp.cos(angles) * weight_scale, -jnp.sin(angles) * weight_scale], axis=0
    ).astype(jnp.bfloat16)
    return table


def exchange(n_lat, n_lev, forward, src_ref, dst_ref, send_sem, recv_sem, own_sem):
    n = n_lat * n_lev
    i = lax.axis_index("lat")
    j = lax.axis_index("lev")
    me = i * n_lev + j
    pairs = 3

    def ends(peer_i, peer_j, peer):
        if forward:
            return src_ref.at[peer], dst_ref.at[:, :, :, j, pl.ds(i * pairs, pairs)]
        return src_ref.at[:, :, peer_j, pl.ds(peer_i * pairs, pairs)], dst_ref.at[me]

    def start(step, carry):
        peer = lax.rem(me + step, n)
        peer_i = peer // n_lev
        peer_j = lax.rem(peer, n_lev)
        src, dst = ends(peer_i, peer_j, peer)
        pltpu.make_async_remote_copy(
            src_ref=src, dst_ref=dst, send_sem=send_sem, recv_sem=recv_sem,
            device_id=(peer_i, peer_j), device_id_type=MESH,
        ).start()
        return carry

    src, dst = ends(i, j, me)
    own = pltpu.make_async_copy(src, dst, own_sem)
    own.start()
    lax.fori_loop(1, n, start, 0)
    own.wait()
    many = (src_ref if forward else dst_ref).at[pl.ds(0, n - 1)]
    pltpu.make_async_copy(many, many, send_sem).wait()
    pltpu.make_async_copy(many, many, recv_sem).wait()


def exchange_call(array, out_shape, n_lat, n_lev, forward):
    return pl.pallas_call(
        functools.partial(exchange, n_lat, n_lev, forward),
        out_shape=jax.ShapeDtypeStruct(out_shape, array.dtype),
        in_specs=[pl.BlockSpec(memory_space=pl.ANY)],
        out_specs=pl.BlockSpec(memory_space=pl.ANY),
        scratch_shapes=[pltpu.SemaphoreType.DMA] * 3,
        compiler_params=pltpu.CompilerParams(has_side_effects=True),
        name="exchange_out" if forward else "exchange_back",
    )(array)


def dot(a, b, dims):
    return lax.dot_general(a, b, (dims, ((), ())), preferred_element_type=jnp.float32)


def sigmoid(z):
    return 0.5 * jnp.tanh(0.5 * z) + 0.5


def join_levels(parts):
    half = parts[0].shape[1] // 2
    rows = []
    for p in range(2):
        rows.append(
            jnp.concatenate([a[:, p * half : (p + 1) * half] for a in parts], axis=1)
        )
    return jnp.concatenate(rows, axis=0)


def column_kernel(
    recv_ref, table_ref, table_t_ref, gain_ref, w_in_ref, b_in_ref, w_mid_ref, b_mid_ref,
    w_out_ref, back_ref, g_gain_ref, g_in_ref, g_b_in_ref, g_mid_ref, g_b_mid_ref, g_out_ref,
):
    first = pl.program_id(0) == 0

    @pl.when(first)
    def _():
        for ref in (g_gain_ref, g_in_ref, g_b_in_ref, g_mid_ref, g_b_mid_ref, g_out_ref):
            ref[...] = jnp.zeros_like(ref)

    levels = recv_ref.shape[3]
    state = join_levels([recv_ref[0, 0, 0, j] for j in range(levels)])
    cot = join_levels([recv_ref[1, 0, 0, j] for j in range(levels)])
    nn, nt, tn = (((1,), (0,)), ((1,), (1,)), ((0,), (0,)))
    columns = dot(table_t_ref[...], state, nn).astype(jnp.bfloat16)
    column_cot = dot(table_t_ref[...], cot, nn).astype(jnp.bfloat16)
    gain = gain_ref[...]
    inputs = columns.astype(jnp.float32)
    inverse = lax.rsqrt(jnp.mean(inputs * inputs, axis=1, keepdims=True) + norm_eps)
    normed = (inputs * inverse * gain).astype(jnp.bfloat16)
    pre_one = dot(normed, w_in_ref[...], nn) + b_in_ref[...]
    sig_one = sigmoid(pre_one)
    act_one = (pre_one * sig_one).astype(jnp.bfloat16)
    slope_one = sig_one * (1.0 + pre_one * (1.0 - sig_one))
    pre_two = dot(act_one, w_mid_ref[...], nn) + b_mid_ref[...]
    sig_two = sigmoid(pre_two)
    act_two = (pre_two * sig_two).astype(jnp.bfloat16)
    slope_two = sig_two * (1.0 + pre_two * (1.0 - sig_two))
    back_two = dot(column_cot, w_out_ref[...], nt)
    delta_two32 = back_two * slope_two
    delta_two = delta_two32.astype(jnp.bfloat16)
    back_one = dot(delta_two, w_mid_ref[...], nt)
    delta_one = (back_one * slope_one).astype(jnp.bfloat16)
    back_norm = dot(delta_one, w_in_ref[...], nt)
    scaled = back_norm * gain
    grad_columns = inverse * scaled - inputs * (inverse * inverse * inverse) * jnp.mean(
        scaled * inputs, axis=1, keepdims=True
    )
    grad_columns = grad_columns.astype(jnp.bfloat16)
    back = dot(table_ref[...], grad_columns, nn).astype(jnp.bfloat16)
    slots = back.shape[0] // 2
    half = back.shape[1] // levels
    for j in range(levels):
        back_ref[0, 0, j] = jnp.concatenate(
            [
                back[p * slots : (p + 1) * slots, j * half : (j + 1) * half]
                for p in range(2)
            ],
            axis=1,
        )
    g_out_ref[...] += dot(act_two, column_cot, tn)
    g_mid_ref[...] += dot(act_one, delta_two, tn)
    g_in_ref[...] += dot(normed, delta_one, tn)
    g_b_mid_ref[...] += jnp.sum(delta_two.astype(jnp.float32), axis=0, keepdims=True)
    g_b_in_ref[...] += jnp.sum(delta_one.astype(jnp.float32), axis=0, keepdims=True)
    g_gain_ref[...] += jnp.sum(back_norm * inputs * inverse, axis=0, keepdims=True)


def column_call(recv, table, gain, w_in, b_in, w_mid, b_mid, w_out):
    kinds, rows, members, levels, slots, lanes = recv.shape
    table_t = table.T
    params = (table, table_t, gain[None], w_in, b_in[None], w_mid, b_mid[None], w_out)
    whole = lambda a: pl.BlockSpec(a.shape, lambda b: (0,) * a.ndim)
    f32 = jnp.float32
    grads = [
        jax.ShapeDtypeStruct(s, f32)
        for s in (
            (1, gain.shape[0]), w_in.shape, (1, b_in.shape[0]), w_mid.shape, (1, b_mid.shape[0]),
            w_out.shape,
        )
    ]
    back = jax.ShapeDtypeStruct((rows, members, levels, slots, lanes), recv.dtype)
    return pl.pallas_call(
        column_kernel,
        grid=(rows * members,),
        out_shape=[back] + grads,
        in_specs=[
            pl.BlockSpec(
                (kinds, 1, 1, levels, slots, lanes),
                lambda b: (0, b // members, b % members, 0, 0, 0),
            )
        ]
        + [whole(a) for a in params],
        out_specs=[
            pl.BlockSpec(
                (1, 1, levels, slots, lanes), lambda b: (b // members, b % members, 0, 0, 0)
            )
        ]
        + [whole(a) for a in grads],
        compiler_params=pltpu.CompilerParams(
            dimension_semantics=("arbitrary",), vmem_limit_bytes=56 * 1024 * 1024
        ),
        name="columns",
    )(recv, *params)


def local(
    n_lat, n_lev, spec_in, cotangent, legendre, quad_weights, wave_order, norm_gain, weight_in,
    bias_in, weight_mid, bias_mid, weight_out,
):
    bf16 = jnp.bfloat16
    n = n_lat * n_lev
    slots_here, degrees, members, lanes = spec_in.shape
    rows = NLAT // n
    own_waves = lax.dynamic_slice_in_dim(wave_order, lax.axis_index("lat") * slots_here, slots_here)
    living, shrink = spectral_masks(own_waves, degrees)
    basis_rows = jnp.where(living[:, :, None], legendre, jnp.zeros_like(legendre))
    table = fourier_tables(wave_order)
    lane = np.arange(lanes)
    apart = np.zeros((lanes, lanes), np.float32)
    apart[lane, (lane % 2) * (lanes // 2) + lane // 2] = 1.0
    apart = jnp.asarray(apart, bf16)

    state = jnp.einsum("slek,kq->sleq", spec_in, apart, preferred_element_type=jnp.float32)
    pushed = (time_step * cotangent.astype(jnp.float32) * shrink[:, :, None, None]).astype(bf16)
    pushed = jnp.einsum("slek,kq->sleq", pushed, apart, preferred_element_type=jnp.float32)
    fourier = jnp.einsum(
        "slt,sleq->steq", basis_rows, state.astype(bf16), preferred_element_type=jnp.float32
    ).astype(bf16)
    pulled = jnp.einsum(
        "slt,sleq->steq", basis_rows, pushed.astype(bf16), preferred_element_type=jnp.float32
    )
    pulled = (quad_weights[None, :, None, None] * pulled).astype(bf16)
    both = jnp.stack([fourier, pulled])
    both = both.reshape(2, slots_here, n, rows, members, lanes).transpose(2, 0, 3, 4, 1, 5)
    both = both.reshape(n, 2, rows, members, slots_here // 2, 2, lanes)
    recv = exchange_call(
        both, (2, rows, members, n_lev, n_lat * slots_here // 2, 2, lanes), n_lat, n_lev, True
    )
    recv = recv.reshape(2, rows, members, n_lev, n_lat * slots_here, lanes)
    back, *grads = column_call(
        recv, table, norm_gain, weight_in, bias_in, weight_mid, bias_mid, weight_out
    )
    back = back.reshape(rows, members, n_lev, n_lat * slots_here // 2, 2, lanes)
    summed = lax.psum(tuple(grads), ("lat", "lev"))
    landed = exchange_call(
        back, (n, rows, members, slots_here // 2, 2, lanes), n_lat, n_lev, False
    )
    landed = landed.reshape(n * rows, members, slots_here, lanes)
    landed = jnp.einsum(
        "tesq,kq->stek", landed, apart, preferred_element_type=jnp.float32
    ).astype(bf16)
    grad_spec = cotangent.astype(jnp.float32) * shrink[:, :, None, None] + jnp.einsum(
        "slt,stek->slek", basis_rows, landed, preferred_element_type=jnp.float32
    )
    factor = float(MEMBERS * NLAT * NLON) ** (-0.5)
    out = [piece * factor for piece in summed]
    return (grad_spec, out[0][0], out[1], out[2][0], out[3], out[4][0], out[5])


def solution(mesh):
    split = P("lat", None, None, "lev")
    placed = (split, split, P("lat", None, None)) + (P(),) * 8
    return jax.shard_map(
        functools.partial(local, mesh.shape["lat"], mesh.shape["lev"]),
        mesh=mesh,
        in_specs=placed,
        out_specs=(split,) + (P(),) * 6,
        check_vma=False,
    )
```

time: 449 us -> 296 us (0.66); the launches traced: 443 us -> 296 us
  Pallas kernels: 0 us -> 122 us
  local copies, waits for them, and re-layouts: 99.6 us -> 15.8 us
  blocking collectives: 132 us -> 66.6 us
  waiting for transfers between devices: 99.6 us -> 57.6 us
  matrix products: 49.6 us -> 7.98 us
  starting transfers between devices: 24.5 us -> 0.04 us
  other arithmetic: 23.3 us -> 11.5 us
    pallas_call x0 -> x3, Pallas kernels: none -> 122 us  [the longest x2 96.7 us: exchange_call(): pl.pallas_call(functools.partial(exchange, n_lat, n_lev, forward), out_sh...]
    all_to_all x1 -> x0, blocking collectives: 55.2 us -> none  [in_one_piece(): lax.all_to_all(both, axis, split_axis=split_dim, concat_axis=concat_dim,...]
    all_to_all x3 -> x0, waiting for transfers between devices: 50.1 us -> none  [the longest x1 38.7 us: in_one_piece(): lax.all_to_all(both, axis, split_axis=split_dim, concat_axis=concat_dim,...]
    dot_general x14 -> x3, matrix products: 49.6 us -> 7.98 us  [the longest x1 3.01 us: local(): jnp.einsum('slt,stek->slek', basis_rows, landed, preferred_element_type=j...]
    all_to_all x3 -> x0, starting transfers between devices: 24.5 us -> none  [the longest x1 11.8 us: in_one_piece(): lax.all_to_all(both, axis, split_axis=split_dim, concat_axis=concat_dim,...]
    all_to_all x5 -> x0, local copies, waits for them, and re-layouts: 20.6 us -> none  [the longest x2 15.5 us: in_one_piece(): lax.all_to_all(both, axis, split_axis=split_dim, concat_axis=concat_dim,...]
    unnamed x41 -> x23, local copies, waits for them, and re-layouts: 21.1 us -> 2.19 us
    concatenate x2 -> x1, local copies, waits for them, and re-layouts: 17.5 us -> 0.96 us  [fourier_tables(): jnp.concatenate([jnp.cos(angles) * weight_scale, -jnp.sin(angles) * weigh...]
  transfers between devices with their start and end apart: 4 -> 1, of which waited for: 3 -> 1; matrix products, arithmetic and copies ran while one was open for 8% -> 4% of each run, Pallas kernels for 0% -> 12%
where the time goes in v1:
time: 296 us
  Pallas kernels  122 us (41%)
  blocking collectives  66.6 us (22%)
  waiting for transfers between devices  57.6 us (19%)
  local copies, waits for them, and re-layouts  15.8 us (5%)
  between operations  14.2 us (5%)
  other arithmetic  11.5 us (4%)
  matrix products  7.98 us (3%)
    pallas_call x2, Pallas kernels, exchange_call(): pl.pallas_call(functools.partial(exchange, n_lat, n_lev, forward), out_sh...  96.7 us
    psum x1, blocking collectives, local(): summed = lax.psum(tuple(grads), ('lat', 'lev'))  66.6 us
    psum x1, waiting for transfers between devices, local(): summed = lax.psum(tuple(grads), ('lat', 'lev'))  57.6 us
    pallas_call x1, Pallas kernels, column_call(): pl.pallas_call(column_kernel, grid=(rows * members,), out_shape=[back] +...  25.4 us
    mul x5, other arithmetic, local(): out = [piece * factor for piece in summed]  6.08 us
  transfers between devices with their start and end apart: 1, of which 1 were waited for; matrix products, arithmetic and copies ran while one was open for 4% of the time, Pallas kernels for 12%

profile of v1, /device:TPU:1, one launch (start us, length us, event | category | flops | bytes accessed | tf_op | source)
XLA Modules:
  0.0 295.9 jit_solution(9711722346713272008)
XLA Ops:
  7.3 0.8 compare_select_fusion
  8.0 3.1 %multiply_convert_fusion.2 = (bf16[192,512]{0,1:T(8,128)(2,1)S(1)}, bf16[192,512]{0,1:T(8,128)(2,1)S(1)}) fusion(f32[192]{0:T(256)S(1)} %compare_select_fusion, s32[192]{0:T(256)} %param.16), kind=kLoop, calls=%fused_computation.28 | loop fusion | flops 1867776 | bytes 394752 | tf_op jit(solution)/shard_map/convert
  11.1 0.9 fusion.41.table_t_ref
  12.0 0.2 pad_maximum_fusion.1
  12.4 1.0 copy.28.table_ref
  13.4 2.4 multiply_convert_fusion
  15.9 1.8 copy.26
  17.7 2.5 convolution_convert_fusion.1
  20.2 1.8 copy.25
  22.0 0.3 pad_maximum_fusion
  22.3 4.9 %copy.27.src_ref = bf16[128,2,2,4,3,2,128]{6,5,4,3,2,1,0:T(2,128)(2,1)} copy(bf16[128,2,2,4,3,2,128]{6,0,5,4,3,2,1:T(8,128)(2,1)S(1)} %bitcast.39) | data formatting | bytes 6291456 | tf_op jit(solution)/shard_map/reshape | solution.py:233
  27.2 60.2 %exchange_out.1 = bf16[2,2,4,4,96,2,128]{6,5,4,3,2,1,0:T(2,128)(2,1)} custom-call(bf16[128,2,2,4,3,2,128]{6,5,4,3,2,1,0:T(2,128)(2,1)} %copy.27.src_ref), custom_call_target="tpu_custom_call" | custom-call | tf_op jit(solution)/shard_map/exchange_out/pallas_call | solution.py:78
  87.4 25.4 %columns.1 = (bf16[2,4,4,192,128]{4,3,2,1,0:T(8,128)(2,1)}, f32[1,256]{1,0:T(1,128)}, f32[256,512]{1,0:T(8,128)}, f32[1,512]{1,0:T(1,128)}, f32[512,512]{1,0:T(8...) custom-call(bf16[2,2,4,4,192,128]{5,4,3,2,1,0:T(8,128)(2,1)} %bitcast.38, bf16[384,512]{1,0:T(8,128)(2,1)} %copy.28.table_ref, ...), custom_call_target="tpu_custom_call" | custom-call | tf_op jit(solution)/shard_map/columns/pallas_call | solution.py:180
  112.9 36.6 %exchange_back.1 = bf16[128,2,4,3,2,128]{5,4,3,2,1,0:T(2,128)(2,1)} custom-call(bf16[2,4,4,96,2,128]{5,4,3,2,1,0:T(2,128)(2,1)} %bitcast.41), custom_call_target="tpu_custom_call" | custom-call | tf_op jit(solution)/shard_map/exchange_back/pallas_call | solution.py:78
  149.4 4.1 %copy.29 = bf16[128,2,4,3,2,128]{5,1,0,4,3,2:T(2,128)(2,1)} copy(bf16[128,2,4,3,2,128]{5,4,3,2,1,0:T(2,128)(2,1)} %exchange_back.1) | data formatting | bytes 3145728 | tf_op jit(solution)/shard_map/exchange_back/pallas_call | solution.py:78
  153.6 3.0 %fusion = f32[6,171,4,128]{3,1,2,0:T(8,128)S(1)} fusion(bf16[128,128,1,1]{1,0,2,3:T(8,128)(2,1)S(1)} %copy-done.10, bf16[256,4,6,128]{3,0,2,1:T(8,128)(2,1)} %bitcast.42, f32[6,171]{1,0:T(8,128)S(1)} %get-tuple-element.43, bf16[6,171,4,128]{3,2,1,0:T(4,128)(2,1)} %param.13, bf16[6,171,256]{2,1,0:T(8,128)(2,1)} %param.14, pred[6,171]{1,0:T(8,128)(4,1)S(1)} %fusion.29), kind=kOutput, calls=%fused_computation.4 | convolution fusion | flops 472911360 | bytes 5287946 | tf_op jit(solution)/shard_map/slt,stek->slek/dot_general | solution.py:250
  156.6 2.1 copy.30
  158.8 66.6 %all-reduce = (f32[1,256]{1,0:T(1,128)S(1)}, f32[1,512]{1,0:T(1,128)S(1)}, f32[1,512]{1,0:T(1,128)S(1)}) all-reduce(f32[1,256]{1,0:T(1,128)S(1)} %copy-done.7, f32[1,512]{1,0:T(1,128)S(1)} %copy-done.5, f32[1,512]{1,0:T(1,128)S(1)} %copy-done.6), channel_id=1, replica_groups=mesh['lat'=32,'lev'=4] {'lat','lev'}, use_global_device_ids=true, to_apply=%region_0.1 | all-reduce | flops 1280 | bytes 10240 | tf_op jit(solution)/shard_map/psum | solution.py:242
  225.4 0.6 broadcast_multiply_fusion.6
  226.0 0.6 broadcast_multiply_fusion.4
  226.6 57.6 %all-reduce.4.cloned.1.call-done = (f32[256,512]{1,0:T(8,128)}, f32[512,512]{1,0:T(8,128)}, f32[512,256]{1,0:T(8,128)}) async-done(((f32[256,512]{1,0:T(8,128)}, f32[512,512]{1,0:T(8,128)}, f32[512,256]{1,0:T(8,128)}), (f32[256,512]{1,0:T(8,128)}, f32[512,512]{1,0:T(8,128)}, f32[512,256]{1,0:T(8,128)})) %all-reduce.4.cloned.1.call-update) | async-done | bytes 2097168 | tf_op jit(solution)/shard_map/psum | solution.py:242
  284.1 2.0 broadcast_multiply_fusion.2
  286.1 1.9 broadcast_multiply_fusion.1
  288.0 1.1 broadcast_multiply_fusion
  (28 shorter events, 0.4 us)
Async XLA Ops:
  7.2 10.5 %copy-start = (bf16[6,171,4,128]{3,2,1,0:T(4,128)(2,1)S(1)}, bf16[6,171,4,128]{3,2,1,0:T(4,128)(2,1)}, u32[]{:S(2)}) copy-start(bf16[6,171,4,128]{3,2,1,0:T(4,128)(2,1)} %param.12) | copy-start | bytes 3151876
  7.2 5.0 %copy-start.4 = (s32[192]{0:T(256)S(1)}, s32[192]{0:T(256)}, u32[]{:S(2)}) copy-start(s32[192]{0:T(256)} %param.16) | copy-start | bytes 2308
  7.2 276.9 %all-reduce.4.cloned.1.call-start = ((), (), s32[]{:S(2)}) async-start(), calls=%async_computation | async-start | bytes 4194304 | tf_op jit(solution)/shard_map/psum | solution.py:242
  8.0 5.4 %copy-start.2 = (bf16[6,171,256]{2,1,0:T(8,128)(2,1)S(1)}, bf16[6,171,256]{2,1,0:T(8,128)(2,1)}, u32[]{:S(2)}) copy-start(bf16[6,171,256]{2,1,0:T(8,128)(2,1)} %param.14) | copy-start | bytes 1575940
  8.0 5.4 %copy-start.3 = (bf16[128,128,1,1]{1,0,3,2:T(8,128)(2,1)S(1)}, bf16[128,128,1,1]{1,0,3,2:T(8,128)(2,1)}, u32[]{:S(2)}) copy-start(bf16[128,128,1,1]{1,0,3,2:T(8,128)(2,1)} %constant.59) | copy-start | bytes 98308
  8.0 5.4 %copy-start.8 = (bf16[6,171,4,128]{3,2,1,0:T(4,128)(2,1)S(1)}, bf16[6,171,4,128]{3,2,1,0:T(4,128)(2,1)}, u32[]{:S(2)}) copy-start(bf16[6,171,4,128]{3,2,1,0:T(4,128)(2,1)} %param.13) | copy-start | bytes 3151876
  8.0 5.4 %copy-start.9 = (f32[256]{0:T(256)S(1)}, f32[256]{0:T(256)}, u32[]{:S(2)}) copy-start(f32[256]{0:T(256)} %param.15) | copy-start | bytes 3076
  149.4 4.2 %copy-start.10 = (bf16[128,128,1,1]{1,0,2,3:T(8,128)(2,1)S(1)}, bf16[128,128,1,1]{1,0,2,3:T(8,128)(2,1)}, u32[]{:S(2)}) copy-start(bf16[128,128,1,1]{1,0,2,3:T(8,128)(2,1)} %constant.60) | copy-start | bytes 98308
  156.6 2.2 copy-start.5
  156.6 2.2 copy-start.6
  156.6 2.2 copy-start.7
  284.1 3.9 %copy-start.1 = (f32[512,512]{1,0:T(8,128)S(1)}, f32[512,512]{1,0:T(8,128)}, u32[]{:S(2)}) copy-start(f32[512,512]{1,0:T(8,128)} %get-tuple-element.39) | copy-start | bytes 3145732
Sparse Core Ops, SparseCore 0:
  113.0 171.1 all-reduce.3

commit v2 on v1

v2 whole, which is shorter than its diff:
```python
import functools
import math

import jax
import jax.numpy as jnp
import numpy as np
from jax import lax
from jax.experimental import pallas as pl
from jax.experimental.pallas import tpu as pltpu
from jax.sharding import PartitionSpec as P

WAVES = 171
NLAT = 256
NLON = 512
MEMBERS = 4

time_step = 0.5
norm_eps = 1e-06
MESH = pl.DeviceIdType.MESH


def spectral_masks(waves_held, degree_count):
    degree = jnp.arange(degree_count, dtype=jnp.int32)
    living = (waves_held[:, None] <= degree[None, :]) & (waves_held[:, None] < WAVES)
    ratio = (degree * (degree + 1)).astype(jnp.float32) / float(WAVES * (WAVES - 1))
    factor = 1.0 / (1.0 + ratio * ratio)
    shrink = jnp.where(living, factor[None, :], jnp.zeros_like(factor)[None, :])
    return (living, shrink)


def fourier_tables(waves_all):
    longitude = jnp.arange(NLON, dtype=jnp.int32)
    phase_steps = waves_all[:, None] * longitude[None, :] % NLON
    angles = phase_steps.astype(jnp.float32) * (2.0 * math.pi / NLON)
    weight_scale = jnp.where(waves_all < WAVES, math.sqrt(2.0 / NLON), 0.0).astype(jnp.float32)[
        :, None
    ]
    table = jnp.concatenate(
        [jnp.cos(angles) * weight_scale, -jnp.sin(angles) * weight_scale], axis=0
    ).astype(jnp.bfloat16)
    return table


def part(value, size, of):
    return lax.rem(value // of, size)


def peer_at(step, i, j):
    away = lax.rem(step * 37, 128)
    z = lax.rem(i // 8 + lax.rem(away, 4), 4)
    y = lax.rem(part(i, 4, 2) + part(away, 4, 4), 4)
    x = lax.rem(lax.rem(i, 2) * 2 + j // 2 + part(away, 4, 16), 4)
    core = lax.rem(j + away // 64, 2)
    return z * 8 + y * 2 + x // 2, lax.rem(x, 2) * 2 + core


def chip_at(step, i, j):
    away = lax.rem(step * 37, 64)
    z = lax.rem(i // 8 + lax.rem(away, 4), 4)
    y = lax.rem(part(i, 4, 2) + part(away, 4, 4), 4)
    x = lax.rem(lax.rem(i, 2) * 2 + j // 2 + away // 16, 4)
    return z * 8 + y * 2 + x // 2, lax.rem(x, 2) * 2 + lax.rem(j, 2)


def send(src, dst, send_sem, recv_sem, peer):
    copy = pltpu.make_async_remote_copy(
        src_ref=src, dst_ref=dst, send_sem=send_sem, recv_sem=recv_sem,
        device_id=peer, device_id_type=MESH,
    )
    copy.start()
    return copy


def await_bytes(like, sem):
    pltpu.make_async_copy(like, like, sem).wait()


def exchange_out(n, src_ref, dst_ref, send_sem, recv_sem, own_sem):
    i, j = lax.axis_index("lat"), lax.axis_index("lev")
    slots, kinds = src_ref.shape[:2]

    def ends(kind, peer):
        return src_ref.at[:, kind, peer], dst_ref.at[kind, j, pl.ds(i * slots, slots)]

    def start(step, carry):
        peer = peer_at(step, i, j)
        for kind in range(kinds):
            send(*ends(kind, peer[0] * 4 + peer[1]), send_sem, recv_sem, peer)
        return carry

    for kind in range(kinds):
        pltpu.make_async_copy(*ends(kind, i * 4 + j), own_sem).start()
    lax.fori_loop(1, n, start, 0)
    await_bytes(src_ref.at[:, :, 0], own_sem)
    many = src_ref.at[:, :, pl.ds(0, n - 1)]
    await_bytes(many, send_sem)
    await_bytes(many, recv_sem)


def exchange_out_call(array, n_lat, n_lev):
    slots, kinds, n, two, lanes = array.shape
    return pl.pallas_call(
        functools.partial(exchange_out, n),
        out_shape=jax.ShapeDtypeStruct((kinds, n_lev, n_lat * slots, two, lanes), array.dtype),
        in_specs=[pl.BlockSpec(memory_space=pl.ANY)],
        out_specs=pl.BlockSpec(memory_space=pl.ANY),
        scratch_shapes=[pltpu.SemaphoreType.DMA] * 3,
        compiler_params=pltpu.CompilerParams(has_side_effects=True),
        name="exchange_out",
    )(array)


def exchange_back(
    n, back_ref, grads_ref, small_ref, landed_ref, total_ref, small_total_ref,
    own_half, their_half, rs_src, rs_recv, ag_src, small_recv, small_sum,
    pair_sems, back_sems, rs_sems, ag_sems, swap_sems, small_sems, small_back_sems, local_sems,
):
    i, j = lax.axis_index("lat"), lax.axis_index("lev")
    me = i * 4 + j
    core = lax.rem(j, 2)
    chip = i * 2 + j // 2
    chips = n // 2
    partner = (i, j + 1 - 2 * core)
    slots = landed_ref.shape[1]
    is_owner = me == 0

    pair = send(grads_ref.at[1 - core], their_half, pair_sems.at[0], pair_sems.at[1], partner)
    own = pltpu.make_async_copy(grads_ref.at[core], own_half, local_sems.at[0])
    own.start()
    stay = pltpu.make_async_copy(
        back_ref.at[:, j, pl.ds(i * slots, slots)], landed_ref.at[:, :, me], local_sems.at[1]
    )
    stay.start()

    @pl.when(jnp.logical_not(is_owner))
    def _():
        send(small_ref, small_recv.at[me], small_sems.at[0], small_sems.at[1], (0, 0))

    def start_back(step, carry):
        peer = peer_at(step, i, j)
        send(
            back_ref.at[:, peer[1], pl.ds(peer[0] * slots, slots)], landed_ref.at[:, :, me],
            back_sems.at[0], back_sems.at[1], peer,
        )
        return carry

    lax.fori_loop(1, n, start_back, 0)

    own.wait()
    pair.wait()
    rs_src[...] = (own_half[...] + their_half[...]).astype(rs_src.dtype).reshape(rs_src.shape)

    def start_rs(step, carry):
        peer = chip_at(step, i, j)
        send(
            rs_src.at[peer[0] * 2 + peer[1] // 2], rs_recv.at[chip],
            rs_sems.at[0], rs_sems.at[1], peer,
        )
        return carry

    lax.fori_loop(1, chips, start_rs, 0)

    @pl.when(is_owner)
    def _():
        mine = pltpu.make_async_copy(small_ref, small_recv.at[0], local_sems.at[2])
        mine.start()
        mine.wait()
        await_bytes(small_recv.at[pl.ds(0, n - 1)], small_sems.at[1])
        small_sum[...] = jnp.sum(small_recv[...], axis=0)

        def start_small(step, carry):
            peer = peer_at(step, i, j)
            send(
                small_sum, small_total_ref, small_back_sems.at[0], small_back_sems.at[1], peer
            )
            return carry

        lax.fori_loop(1, n, start_small, 0)
        mine = pltpu.make_async_copy(small_sum, small_total_ref, local_sems.at[2])
        mine.start()
        mine.wait()
        await_bytes(small_recv.at[pl.ds(0, n - 1)], small_back_sems.at[0])

    @pl.when(jnp.logical_not(is_owner))
    def _():
        await_bytes(small_ref, small_sems.at[0])

    rs_recv[chip] = rs_src[chip]
    await_bytes(rs_src.at[pl.ds(0, chips - 1)], rs_sems.at[1])
    ag_src[...] = jnp.sum(rs_recv[...].astype(jnp.float32), axis=0).astype(ag_src.dtype)

    def start_ag(step, carry):
        peer = chip_at(step, i, j)
        send(ag_src, total_ref.at[core, chip], ag_sems.at[0], ag_sems.at[1], peer)
        return carry

    lax.fori_loop(1, chips, start_ag, 0)
    mine = pltpu.make_async_copy(ag_src, total_ref.at[core, chip], local_sems.at[3])
    mine.start()
    mine.wait()
    await_bytes(rs_src.at[pl.ds(0, chips - 1)], rs_sems.at[0])
    await_bytes(rs_src.at[pl.ds(0, chips - 1)], ag_sems.at[1])
    swap = send(
        total_ref.at[core], total_ref.at[core], swap_sems.at[0], swap_sems.at[1], partner
    )
    await_bytes(rs_src.at[pl.ds(0, chips - 1)], ag_sems.at[0])
    stay.wait()
    many = landed_ref.at[:, :, pl.ds(0, n - 1)]
    await_bytes(many, back_sems.at[0])
    await_bytes(many, back_sems.at[1])

    @pl.when(jnp.logical_not(is_owner))
    def _():
        await_bytes(small_ref, small_back_sems.at[1])

    swap.wait()


def exchange_back_call(back, grads, small, n_lat, n_lev):
    members, _, all_slots, two, lanes = back.shape
    n = n_lat * n_lev
    bf16 = jnp.bfloat16
    grads = grads.reshape(2, -1, lanes)
    half = grads.shape[1]
    chips = n // 2
    slices = (chips, half // chips, lanes)
    return pl.pallas_call(
        functools.partial(exchange_back, n),
        out_shape=(
            jax.ShapeDtypeStruct((members, all_slots // n_lat, n, two, lanes), back.dtype),
            jax.ShapeDtypeStruct((2,) + slices, bf16),
            jax.ShapeDtypeStruct(small.shape, small.dtype),
        ),
        in_specs=[pl.BlockSpec(memory_space=pl.ANY)] * 3,
        out_specs=[pl.BlockSpec(memory_space=pl.ANY)] * 3,
        scratch_shapes=[
            pltpu.VMEM((half, lanes), jnp.float32),
            pltpu.VMEM((half, lanes), jnp.float32),
            pltpu.VMEM(slices, bf16),
            pltpu.VMEM(slices, bf16),
            pltpu.VMEM(slices[1:], bf16),
            pltpu.VMEM((n,) + small.shape, small.dtype),
            pltpu.VMEM(small.shape, small.dtype),
        ]
        + [pltpu.SemaphoreType.DMA((2,))] * 7
        + [pltpu.SemaphoreType.DMA((4,))],
        compiler_params=pltpu.CompilerParams(has_side_effects=True),
        name="exchange_back",
    )(back, grads, small)


def dot(a, b, dims):
    return lax.dot_general(a, b, (dims, ((), ())), preferred_element_type=jnp.float32)


def sigmoid(z):
    return 0.5 * jnp.tanh(0.5 * z) + 0.5


def join_levels(parts):
    half = parts[0].shape[1] // 2
    rows = []
    for p in range(2):
        rows.append(
            jnp.concatenate([a[:, p * half : (p + 1) * half] for a in parts], axis=1)
        )
    return jnp.concatenate(rows, axis=0)


def one_of_two(shape, long_dim, which):
    long = lax.broadcasted_iota(jnp.int32, shape, long_dim)
    short = lax.broadcasted_iota(jnp.int32, shape, 1 - long_dim)
    return jnp.where(long == 2 * short + which, 1.0, 0.0).astype(jnp.bfloat16)


NN, NT, TN = (((1,), (0,)), ((1,), (1,)), ((0,), (0,)))


def add_blocks(ref, start, value):
    rows, lanes = value.shape[0], ref.shape[1]
    for b in range(value.shape[1] // lanes):
        ref[pl.ds(start + b * rows, rows)] += value[:, b * lanes : (b + 1) * lanes]


def column_kernel(
    recv_ref, table_ref, table_t_ref, gain_ref, w_in_ref, b_in_ref, w_mid_ref, b_mid_ref,
    w_out_ref, back_ref, grads_ref, small_ref, syn_ref, ana_ref,
):
    waves, longitudes = table_ref.shape

    @pl.when(pl.program_id(0) == 0)
    def _():
        grads_ref[...] = jnp.zeros_like(grads_ref)
        small_ref[...] = jnp.zeros_like(small_ref)
        for r in range(2):
            span = pl.ds(r * longitudes, longitudes)
            syn_ref[span] = dot(
                table_t_ref[...], one_of_two((waves, 2 * waves), 1, r), NN
            ).astype(jnp.bfloat16)
            ana_ref[:, span] = dot(
                one_of_two((2 * waves, waves), 0, r), table_ref[...], NN
            ).astype(jnp.bfloat16)

    levels = recv_ref.shape[2]
    state = join_levels([recv_ref[0, 0, j] for j in range(levels)])
    cot = join_levels([recv_ref[1, 0, j] for j in range(levels)])
    columns = dot(syn_ref[...], state, NN).astype(jnp.bfloat16)
    column_cot = dot(syn_ref[...], cot, NN).astype(jnp.bfloat16)
    gain = gain_ref[...]
    inputs = columns.astype(jnp.float32)
    inverse = lax.rsqrt(jnp.mean(inputs * inputs, axis=1, keepdims=True) + norm_eps)
    normed = (inputs * inverse * gain).astype(jnp.bfloat16)
    pre_one = dot(normed, w_in_ref[...], NN) + b_in_ref[...]
    sig_one = sigmoid(pre_one)
    act_one = (pre_one * sig_one).astype(jnp.bfloat16)
    slope_one = sig_one * (1.0 + pre_one * (1.0 - sig_one))
    pre_two = dot(act_one, w_mid_ref[...], NN) + b_mid_ref[...]
    sig_two = sigmoid(pre_two)
    act_two = (pre_two * sig_two).astype(jnp.bfloat16)
    slope_two = sig_two * (1.0 + pre_two * (1.0 - sig_two))
    back_two = dot(column_cot, w_out_ref[...], NT)
    delta_two = (back_two * slope_two).astype(jnp.bfloat16)
    back_one = dot(delta_two, w_mid_ref[...], NT)
    delta_one = (back_one * slope_one).astype(jnp.bfloat16)
    back_norm = dot(delta_one, w_in_ref[...], NT)
    scaled = back_norm * gain
    grad_columns = inverse * scaled - inputs * (inverse * inverse * inverse) * jnp.mean(
        scaled * inputs, axis=1, keepdims=True
    )
    grad_columns = grad_columns.astype(jnp.bfloat16)
    back = dot(ana_ref[...], grad_columns, NN).astype(jnp.bfloat16)
    half = back.shape[1] // levels
    for j in range(levels):
        back_ref[0, j] = jnp.concatenate(
            [back[p * waves : (p + 1) * waves, j * half : (j + 1) * half] for p in range(2)],
            axis=1,
        )
    first, second = w_in_ref.size // 128, w_mid_ref.size // 128
    add_blocks(grads_ref, 0, dot(normed, delta_one, TN))
    add_blocks(grads_ref, first, dot(act_one, delta_two, TN))
    add_blocks(grads_ref, first + second, dot(act_two, column_cot, TN))
    small = (
        jnp.sum(back_norm * inputs * inverse, axis=0, keepdims=True),
        jnp.sum(delta_one.astype(jnp.float32), axis=0, keepdims=True),
        jnp.sum(delta_two.astype(jnp.float32), axis=0, keepdims=True),
    )
    at = 0
    for value in small:
        add_blocks(small_ref, at, value)
        at += value.shape[1] // 128


def column_call(recv, table, gain, w_in, b_in, w_mid, b_mid, w_out):
    kinds, members, levels, pairs, lanes = recv.shape
    bf16 = jnp.bfloat16
    waves, longitudes = table.shape
    params = (table, table.T, gain[None], w_in, b_in[None], w_mid, b_mid[None], w_out)
    whole = lambda a: pl.BlockSpec(a.shape, lambda b: (0,) * a.ndim)
    out = (
        jax.ShapeDtypeStruct((members, levels, pairs, lanes), bf16),
        jax.ShapeDtypeStruct(
            ((w_in.size + w_mid.size + w_out.size) // lanes, lanes), jnp.float32
        ),
        jax.ShapeDtypeStruct((16, lanes), jnp.float32),
    )
    return pl.pallas_call(
        column_kernel,
        grid=(members,),
        out_shape=out,
        in_specs=[
            pl.BlockSpec((kinds, 1, levels, pairs, lanes), lambda b: (0, b, 0, 0, 0))
        ]
        + [whole(a) for a in params],
        out_specs=[
            pl.BlockSpec((1, levels, pairs, lanes), lambda b: (b, 0, 0, 0)),
            whole(out[1]),
            whole(out[2]),
        ],
        scratch_shapes=[
            pltpu.VMEM((2 * longitudes, 2 * waves), bf16),
            pltpu.VMEM((2 * waves, 2 * longitudes), bf16),
        ],
        compiler_params=pltpu.CompilerParams(
            dimension_semantics=("arbitrary",), vmem_limit_bytes=58 * 1024 * 1024
        ),
        name="columns",
    )(recv, *params)


def local(
    n_lat, n_lev, spec_in, cotangent, legendre, quad_weights, wave_order, norm_gain, weight_in,
    bias_in, weight_mid, bias_mid, weight_out,
):
    bf16 = jnp.bfloat16
    n = n_lat * n_lev
    slots_here, degrees, members, lanes = spec_in.shape
    rows = NLAT // n
    own_waves = lax.dynamic_slice_in_dim(wave_order, lax.axis_index("lat") * slots_here, slots_here)
    living, shrink = spectral_masks(own_waves, degrees)
    basis_rows = jnp.where(living[:, :, None], legendre, jnp.zeros_like(legendre))
    table = fourier_tables(wave_order)
    lane = np.arange(lanes)
    apart = np.zeros((lanes, lanes), np.float32)
    apart[lane, (lane % 2) * (lanes // 2) + lane // 2] = 1.0
    apart = jnp.asarray(apart, bf16)

    pushed = (time_step * cotangent.astype(jnp.float32) * shrink[:, :, None, None]).astype(bf16)
    both = jnp.concatenate([spec_in, pushed], axis=2)
    both = jnp.einsum("slek,kq->sleq", both, apart, preferred_element_type=jnp.float32)
    fourier = jnp.einsum(
        "slt,sleq->setq", basis_rows, both.astype(bf16), preferred_element_type=jnp.float32
    )
    is_state = jnp.arange(2 * members) < members
    weights = jnp.where(is_state[:, None], 1.0, quad_weights[None, :])
    fourier = (fourier * weights[None, :, :, None]).astype(bf16)
    fourier = fourier.reshape(slots_here, 2 * members, n, rows, lanes)
    recv = exchange_out_call(fourier, n_lat, n_lev)
    recv = recv.reshape(2, members, n_lev, n_lat * slots_here * rows, lanes)
    back, grads, small = column_call(
        recv, table, norm_gain, weight_in, bias_in, weight_mid, bias_mid, weight_out
    )
    back = back.reshape(members, n_lev, n_lat * slots_here, rows, lanes)
    landed, total, small = exchange_back_call(back, grads, small, n_lat, n_lev)
    landed = landed.reshape(members, slots_here, n * rows, lanes)
    landed = jnp.einsum(
        "estq,kq->setk", landed, apart, preferred_element_type=jnp.float32
    ).astype(bf16)
    grad_spec = cotangent.astype(jnp.float32) * shrink[:, :, None, None] + jnp.einsum(
        "slt,setk->slek", basis_rows, landed, preferred_element_type=jnp.float32
    )
    factor = float(MEMBERS * NLAT * NLON) ** (-0.5)
    total = total.reshape(-1, lanes)
    out, at = [], 0
    for like in (weight_in, weight_mid, weight_out):
        size = like.size // lanes
        blocks = total[at : at + size].reshape(-1, like.shape[0], lanes)
        out.append(blocks.transpose(1, 0, 2).reshape(like.shape).astype(jnp.float32) * factor)
        at += size
    small = small.reshape(-1) * factor
    gain_end, in_end = norm_gain.size, norm_gain.size + bias_in.size
    return (
        grad_spec, small[:gain_end], out[0], small[gain_end:in_end], out[1],
        small[in_end : in_end + bias_mid.size], out[2],
    )


def solution(mesh):
    split = P("lat", None, None, "lev")
    placed = (split, split, P("lat", None, None)) + (P(),) * 8
    return jax.shard_map(
        functools.partial(local, mesh.shape["lat"], mesh.shape["lev"]),
        mesh=mesh,
        in_specs=placed,
        out_specs=(split,) + (P(),) * 6,
        check_vma=False,
    )
```

time: 296 us -> 154 us (0.52)
  blocking collectives: 66.6 us -> 0 us
  waiting for transfers between devices: 57.6 us -> 0 us
  between operations: 14.2 us -> 0.75 us
  Pallas kernels: 122 us -> 126 us
  local copies, waits for them, and re-layouts: 15.8 us -> 12.3 us
    psum x1 -> x0, blocking collectives: 66.6 us -> none  [local(): summed = lax.psum(tuple(grads), ('lat', 'lev'))]
    psum x1 -> x0, waiting for transfers between devices: 57.6 us -> none  [local(): summed = lax.psum(tuple(grads), ('lat', 'lev'))]
    mul x5 -> x3, other arithmetic: 6.08 us -> 0.86 us  [the longest x1 0.7 us: local(): small = small.reshape(-1) * factor]
    reshape x1 -> x0, local copies, waits for them, and re-layouts: 4.92 us -> none  [local(): both = both.reshape(n, 2, rows, members, slots_here // 2, 2, lanes)]
    pallas_call x1 -> x0, local copies, waits for them, and re-layouts: 4.14 us -> none  [exchange_call(): pl.pallas_call(functools.partial(exchange, n_lat, n_lev, forward), out_sh...]
    pallas_call x3, Pallas kernels: 122 us -> 126 us  [the longest x1 52.2 us: exchange_out_call(): pl.pallas_call(functools.partial(exchange_out, n), out_shape=jax.ShapeDty...]
    unnamed x23 -> x17, local copies, waits for them, and re-layouts: 2.19 us -> 6 us
    another operation x2 -> x0, local copies, waits for them, and re-layouts: 3.57 us -> none  [local(): both = jnp.stack([fourier, pulled])]
  transfers between devices with their start and end apart: 1 -> 0, of which waited for: 1 -> 0; matrix products, arithmetic and copies ran while one was open for 4% -> 0% of each run, Pallas kernels for 12% -> 0%
where the time goes in v2:
time: 154 us
  Pallas kernels  126 us (82%)
  local copies, waits for them, and re-layouts  12.3 us (8%)
  other arithmetic  8.57 us (6%)
  matrix products  6.22 us (4%)
    pallas_call x1, Pallas kernels, exchange_out_call(): pl.pallas_call(functools.partial(exchange_out, n), out_shape=jax.ShapeDty...  52.2 us
    pallas_call x1, Pallas kernels, exchange_back_call(): pl.pallas_call(functools.partial(exchange_back, n), out_shape=(jax.ShapeD...  46.4 us
    pallas_call x1, Pallas kernels, column_call(): pl.pallas_call(column_kernel, grid=(members,), out_shape=out, in_specs=[p...  27.4 us
    unnamed x17, local copies, waits for them, and re-layouts  6 us
    dot_general x1, matrix products, local(): jnp.einsum('slt,sleq->setq', basis_rows, both.astype(bf16), preferred_ele...  3.51 us

profile of v2, /device:TPU:1, one launch (start us, length us, event | category | flops | bytes accessed | tf_op | source)
XLA Modules:
  0.0 153.9 jit_solution(9727321750605014188)
XLA Ops:
  0.7 0.8 broadcast_compare_fusion
  1.5 0.7 compare_select_fusion
  2.3 0.8 broadcast_select_fusion.3
  3.1 3.0 %multiply_convert_fusion.2 = (bf16[192,512]{0,1:T(8,128)(2,1)S(1)}, bf16[192,512]{0,1:T(8,128)(2,1)S(1)}) fusion(f32[192]{0:T(256)S(1)} %compare_select_fusion, s32[192]{0:T(256)} %param.16), kind=kLoop, calls=%fused_computation.30 | loop fusion | flops 1867776 | bytes 394752 | tf_op jit(solution)/shard_map/convert
  6.1 0.9 fusion.40.table_t_ref
  7.1 0.9 copy.22.table_ref
  8.1 1.3 fusion.2
  9.3 1.1 copy.20
  10.5 3.5 %fusion = bf16[6,8,256,128]{2,3,1,0:T(8,128)(2,1)S(1)} fusion(f32[8,256]{1,0:T(8,128)S(1)} %broadcast_select_fusion.3, bf16[128,128,1,1]{1,0,3,2:T(8,128)(2,1)S(1)} %copy-done.5, bf16[6,171,4,128]{3,1,2,0:T(8,128)(2,1)} %fusion.2, bf16[6,171,4,128]{3,1,2,0:T(8,128)(2,1)} %copy.20, bf16[6,171,256]{2,1,0:T(8,128)(2,1)} %param.14, pred[6,171]{1,0:T(8,128)(4,1)S(1)} %fusion.28), kind=kOutput, calls=%fused_computation.1 | convolution fusion | flops 812388864 | bytes 5814274 | tf_op jit(solution)/shard_map/slt,sleq->setq/dot_general | solution.py:410
  14.0 2.8 %copy.21 = bf16[6,8,256,128]{3,2,1,0:T(8,128)(2,1)} copy(bf16[6,8,256,128]{2,3,1,0:T(8,128)(2,1)S(1)} %fusion) | data formatting | bytes 6291456 | tf_op jit(solution)/shard_map/convert_element_type | solution.py:415
  16.8 52.2 %exchange_out.1 = bf16[8,4,192,2,128]{4,3,2,1,0:T(2,128)(2,1)} custom-call(bf16[6,8,128,2,128]{4,3,2,1,0:T(2,128)(2,1)} %bitcast.53), custom_call_target="tpu_custom_call" | custom-call | tf_op jit(solution)/shard_map/exchange_out/pallas_call | solution.py:102
  69.0 27.4 %columns.1 = (bf16[4,4,384,128]{3,2,1,0:T(8,128)(2,1)}, f32[4096,128]{1,0:T(8,128)}, f32[16,128]{1,0:T(8,128)}) custom-call(bf16[2,4,4,384,128]{4,3,2,1,0:T(8,128)(2,1)} %bitcast.52, bf16[384,512]{1,0:T(8,128)(2,1)} %copy.22.table_ref, bf16[512,384]{1,0:T(8,128)(2,1)} %fusion.40.table_t_ref, f32[1,256]{1,0:T(1,128)} %bitcast.69, bf16[256,512]{1,0:T(8,128)(2,1)} %w_in_ref.1, ...), custom_call_target="tpu_custom_call" | custom-call | tf_op jit(solution)/shard_map/columns/pallas_call | solution.py:366
  96.4 46.4 %exchange_back.1 = (bf16[4,6,128,2,128]{4,3,2,1,0:T(2,128)(2,1)}, bf16[2,64,32,128]{3,2,1,0:T(8,128)(2,1)}, f32[16,128]{1,0:T(8,128)}) custom-call(bf16[4,4,192,2,128]{4,3,2,1,0:T(2,128)(2,1)} %bitcast.61, f32[2,2048,128]{2,1,0:T(8,128)} %bitcast.56, f32[16,128]{1,0:T(8,128)} %get-tuple-element.15.small_ref), custom_call_target="tpu_custom_call" | custom-call | tf_op jit(solution)/shard_map/exchange_back/pallas_call | solution.py:227
  142.8 0.7 broadcast_multiply_fusion
  143.5 0.6 slice_bitcast_fusion.2
  144.1 0.6 slice_bitcast_fusion
  144.7 2.7 %fusion.1 = f32[6,171,4,128]{3,1,2,0:T(8,128)S(1)} fusion(bf16[128,128,1,1]{1,0,2,3:T(8,128)(2,1)S(1)} %copy-done.4, bf16[4,6,256,128]{3,2,1,0:T(8,128)(2,1)} %bitcast.70, f32[6,171]{1,0:T(8,128)S(1)} %get-tuple-element.32, bf16[6,171,4,128]{3,2,1,0:T(4,128)(2,1)S(1)} %copy-done.2, bf16[6,171,256]{2,1,0:T(8,128)(2,1)} %param.14, pred[6,171]{1,0:T(8,128)(4,1)S(1)} %fusion.28), kind=kOutput, calls=%fused_computation.4 | convolution fusion | flops 472911360 | bytes 5287946 | tf_op jit(solution)/shard_map/slt,setk->slek/dot_general | solution.py:428
  147.4 2.1 %copy.26 = f32[6,171,4,128]{3,2,1,0:T(4,128)} copy(f32[6,171,4,128]{3,1,2,0:T(8,128)S(1)} %fusion.1) | data formatting | bytes 4202496
  149.6 0.7 copy.24
  150.3 1.0 copy.44
  151.4 0.4 copy.25
  151.9 0.8 copy.45
  152.7 0.3 copy.23
  153.0 0.8 copy.46
  (19 shorter events, 0.5 us)
Async XLA Ops:
  0.6 7.4 %copy-start.1 = (bf16[6,171,4,128]{3,2,1,0:T(4,128)(2,1)S(1)}, bf16[6,171,4,128]{3,2,1,0:T(4,128)(2,1)}, u32[]{:S(2)}) copy-start(bf16[6,171,4,128]{3,2,1,0:T(4,128)(2,1)} %param.13) | copy-start | bytes 3151876
  7.0 2.4 %copy-start = (bf16[6,171,4,128]{3,2,1,0:T(4,128)(2,1)S(1)}, bf16[6,171,4,128]{3,2,1,0:T(4,128)(2,1)}, u32[]{:S(2)}) copy-start(bf16[6,171,4,128]{3,2,1,0:T(4,128)(2,1)} %param.12) | copy-start | bytes 3151876
  8.1 2.4 %copy-start.5 = (bf16[128,128,1,1]{1,0,3,2:T(8,128)(2,1)S(1)}, bf16[128,128,1,1]{1,0,3,2:T(8,128)(2,1)}, u32[]{:S(2)}) copy-start(bf16[128,128,1,1]{1,0,3,2:T(8,128)(2,1)} %constant.61) | copy-start | bytes 98308
  96.4 48.3 %copy-start.2 = (bf16[6,171,4,128]{3,2,1,0:T(4,128)(2,1)S(1)}, bf16[6,171,4,128]{3,2,1,0:T(4,128)(2,1)}, u32[]{:S(2)}) copy-start(bf16[6,171,4,128]{3,2,1,0:T(4,128)(2,1)} %param.13) | copy-start | bytes 3151876
  96.4 48.3 %copy-start.4 = (bf16[128,128,1,1]{1,0,2,3:T(8,128)(2,1)S(1)}, bf16[128,128,1,1]{1,0,2,3:T(8,128)(2,1)}, u32[]{:S(2)}) copy-start(bf16[128,128,1,1]{1,0,2,3:T(8,128)(2,1)} %constant.62) | copy-start | bytes 98308
  147.4 2.1 %copy-start.3 = (bf16[2,64,32,128]{3,2,1,0:T(8,128)(2,1)S(1)}, bf16[2,64,32,128]{3,2,1,0:T(8,128)(2,1)}, u32[]{:S(2)}) copy-start(bf16[2,64,32,128]{3,2,1,0:T(8,128)(2,1)} %get-tuple-element.18) | copy-start | bytes 3145732

commit v3 on v2

v3 whole, which is shorter than its diff:
```python
import functools
import math

import jax
import jax.numpy as jnp
import numpy as np
from jax import lax
from jax.experimental import pallas as pl
from jax.experimental.pallas import tpu as pltpu
from jax.sharding import PartitionSpec as P

WAVES = 171
NLAT = 256
NLON = 512
MEMBERS = 4

time_step = 0.5
norm_eps = 1e-06
MESH = pl.DeviceIdType.MESH


def spectral_masks(waves_held, degree_count):
    degree = jnp.arange(degree_count, dtype=jnp.int32)
    living = (waves_held[:, None] <= degree[None, :]) & (waves_held[:, None] < WAVES)
    ratio = (degree * (degree + 1)).astype(jnp.float32) / float(WAVES * (WAVES - 1))
    factor = 1.0 / (1.0 + ratio * ratio)
    shrink = jnp.where(living, factor[None, :], jnp.zeros_like(factor)[None, :])
    return (living, shrink)


def fourier_tables(waves_all):
    longitude = jnp.arange(NLON, dtype=jnp.int32)
    phase_steps = waves_all[:, None] * longitude[None, :] % NLON
    angles = phase_steps.astype(jnp.float32) * (2.0 * math.pi / NLON)
    weight_scale = jnp.where(waves_all < WAVES, math.sqrt(2.0 / NLON), 0.0).astype(jnp.float32)[
        :, None
    ]
    table = jnp.concatenate(
        [jnp.cos(angles) * weight_scale, -jnp.sin(angles) * weight_scale], axis=0
    ).astype(jnp.bfloat16)
    return table


def part(value, size, of):
    return lax.rem(value // of, size)


def peer_at(step, i, j):
    away = lax.rem(step * 37, 128)
    z = lax.rem(i // 8 + lax.rem(away, 4), 4)
    y = lax.rem(part(i, 4, 2) + part(away, 4, 4), 4)
    x = lax.rem(lax.rem(i, 2) * 2 + j // 2 + part(away, 4, 16), 4)
    core = lax.rem(j + away // 64, 2)
    return z * 8 + y * 2 + x // 2, lax.rem(x, 2) * 2 + core


def chip_at(step, i, j):
    away = lax.rem(step * 37, 64)
    z = lax.rem(i // 8 + lax.rem(away, 4), 4)
    y = lax.rem(part(i, 4, 2) + part(away, 4, 4), 4)
    x = lax.rem(lax.rem(i, 2) * 2 + j // 2 + away // 16, 4)
    return z * 8 + y * 2 + x // 2, lax.rem(x, 2) * 2 + lax.rem(j, 2)


def send(src, dst, send_sem, recv_sem, peer):
    copy = pltpu.make_async_remote_copy(
        src_ref=src, dst_ref=dst, send_sem=send_sem, recv_sem=recv_sem,
        device_id=peer, device_id_type=MESH,
    )
    copy.start()
    return copy


def await_bytes(like, sem):
    pltpu.make_async_copy(like, like, sem).wait()


def dot(a, b, dims):
    return lax.dot_general(a, b, (dims, ((), ())), preferred_element_type=jnp.float32)


def sigmoid(z):
    return 0.5 * jnp.tanh(0.5 * z) + 0.5


def join_levels(parts):
    half = parts[0].shape[1] // 2
    rows = []
    for p in range(2):
        rows.append(
            jnp.concatenate([a[:, p * half : (p + 1) * half] for a in parts], axis=1)
        )
    return jnp.concatenate(rows, axis=0)


def one_of_two(shape, long_dim, which):
    long = lax.broadcasted_iota(jnp.int32, shape, long_dim)
    short = lax.broadcasted_iota(jnp.int32, shape, 1 - long_dim)
    return jnp.where(long == 2 * short + which, 1.0, 0.0).astype(jnp.bfloat16)


NN, NT, TN = (((1,), (0,)), ((1,), (1,)), ((0,), (0,)))


def add_blocks(ref, start, value):
    rows, lanes = value.shape[0], ref.shape[1]
    for b in range(value.shape[1] // lanes):
        ref[pl.ds(start + b * rows, rows)] += value[:, b * lanes : (b + 1) * lanes]


def column_work(
    state, cot, syn_ref, ana_ref, gain_ref, w_in_ref, b_in_ref, w_mid_ref, b_mid_ref, w_out_ref
):
    bf16 = jnp.bfloat16
    columns = dot(syn_ref[...], state, NN).astype(bf16)
    column_cot = dot(syn_ref[...], cot, NN).astype(bf16)
    gain = gain_ref[...]
    inputs = columns.astype(jnp.float32)
    inverse = lax.rsqrt(jnp.mean(inputs * inputs, axis=1, keepdims=True) + norm_eps)
    normed = (inputs * inverse * gain).astype(bf16)
    pre_one = dot(normed, w_in_ref[...], NN) + b_in_ref[...]
    sig_one = sigmoid(pre_one)
    act_one = (pre_one * sig_one).astype(bf16)
    slope_one = sig_one * (1.0 + pre_one * (1.0 - sig_one))
    pre_two = dot(act_one, w_mid_ref[...], NN) + b_mid_ref[...]
    sig_two = sigmoid(pre_two)
    act_two = (pre_two * sig_two).astype(bf16)
    slope_two = sig_two * (1.0 + pre_two * (1.0 - sig_two))
    back_two = dot(column_cot, w_out_ref[...], NT)
    delta_two = (back_two * slope_two).astype(bf16)
    back_one = dot(delta_two, w_mid_ref[...], NT)
    delta_one = (back_one * slope_one).astype(bf16)
    back_norm = dot(delta_one, w_in_ref[...], NT)
    scaled = back_norm * gain
    grad_columns = inverse * scaled - inputs * (inverse * inverse * inverse) * jnp.mean(
        scaled * inputs, axis=1, keepdims=True
    )
    back = dot(ana_ref[...], grad_columns.astype(bf16), NN).astype(bf16)
    gain_sum = jnp.sum(back_norm * inputs * inverse, axis=0, keepdims=True)
    return back, (normed, delta_one, act_one, delta_two, act_two, column_cot, gain_sum)


def whole_step(
    n, four_ref, table_ref, table_t_ref, gain_ref, w_in_ref, b_in_ref, w_mid_ref, b_mid_ref,
    w_out_ref, landed_ref, total_ref, small_total_ref,
    recv_ref, back_ref, syn_ref, ana_ref, grads_ref, small_ref,
    their_half, rs_src, rs_recv, ag_src, small_recv, small_sum,
    out_sems, arrive_sems, own_sems, pair_sems, back_sems, rs_sems, ag_sems, swap_sems,
    small_sems, small_back_sems, local_sems,
):
    i, j = lax.axis_index("lat"), lax.axis_index("lev")
    me = i * 4 + j
    core = lax.rem(j, 2)
    chip = i * 2 + j // 2
    chips = n // 2
    partner = (i, j + 1 - 2 * core)
    members, slots = landed_ref.shape[:2]
    levels = recv_ref.shape[2]
    waves, longitudes = table_ref.shape
    is_owner = me == 0

    def arriving(e):
        return recv_ref.at[e, :, j, pl.ds(i * slots, slots)]

    def start_out(e):
        def start(step, carry):
            peer = peer_at(step, i, j)
            send(
                four_ref.at[e, :, :, peer[0] * 4 + peer[1]], arriving(e),
                out_sems.at[0], arrive_sems.at[e], peer,
            )
            return carry

        pltpu.make_async_copy(four_ref.at[e, :, :, me], arriving(e), own_sems.at[e]).start()
        lax.fori_loop(1, n, start, 0)

    start_out(0)
    start_out(1)
    grads_ref[...] = jnp.zeros_like(grads_ref)
    small_ref[...] = jnp.zeros_like(small_ref)
    for r in range(2):
        span = pl.ds(r * longitudes, longitudes)
        syn_ref[span] = dot(
            table_t_ref[...], one_of_two((waves, 2 * waves), 1, r), NN
        ).astype(jnp.bfloat16)
        ana_ref[:, span] = dot(
            one_of_two((2 * waves, waves), 0, r), table_ref[...], NN
        ).astype(jnp.bfloat16)

    recv_rows = recv_ref.reshape(members, 2, levels, 2 * n // 4 * slots, recv_ref.shape[-1])
    back_rows = back_ref.reshape(members, levels, 2 * n // 4 * slots, back_ref.shape[-1])

    def member(e, carry):
        @pl.when(e < members - 2)
        def _():
            start_out(e + 2)

        pltpu.make_async_copy(four_ref.at[e, :, :, me], arriving(e), own_sems.at[e]).wait()
        await_bytes(four_ref.at[e, :, :, pl.ds(0, n - 1)], arrive_sems.at[e])
        state = join_levels([recv_rows[e, 0, k] for k in range(levels)])
        cot = join_levels([recv_rows[e, 1, k] for k in range(levels)])
        back, rest = column_work(
            state, cot, syn_ref, ana_ref, gain_ref, w_in_ref, b_in_ref, w_mid_ref, b_mid_ref,
            w_out_ref,
        )
        half = back.shape[1] // levels
        for k in range(levels):
            back_rows[e, k] = jnp.concatenate(
                [back[p * waves : (p + 1) * waves, k * half : (k + 1) * half] for p in range(2)],
                axis=1,
            )

        def start_back(step, carry):
            peer = peer_at(step, i, j)
            send(
                back_ref.at[e, peer[1], pl.ds(peer[0] * slots, slots)], landed_ref.at[e, :, me],
                back_sems.at[0], back_sems.at[1], peer,
            )
            return carry

        pltpu.make_async_copy(
            back_ref.at[e, j, pl.ds(i * slots, slots)], landed_ref.at[e, :, me],
            local_sems.at[1],
        ).start()
        lax.fori_loop(1, n, start_back, 0)

        normed, delta_one, act_one, delta_two, act_two, column_cot, gain_sum = rest
        first, second = w_in_ref.size // 128, w_mid_ref.size // 128
        add_blocks(grads_ref, 0, dot(normed, delta_one, TN))
        add_blocks(grads_ref, first, dot(act_one, delta_two, TN))
        add_blocks(grads_ref, first + second, dot(act_two, column_cot, TN))
        at = 0
        for value in (
            gain_sum,
            jnp.sum(delta_one.astype(jnp.float32), axis=0, keepdims=True),
            jnp.sum(delta_two.astype(jnp.float32), axis=0, keepdims=True),
        ):
            add_blocks(small_ref, at, value)
            at += value.shape[1] // 128
        return carry

    lax.fori_loop(0, members, member, 0)

    half_rows = their_half.shape[0]
    pair = send(
        grads_ref.at[pl.ds((1 - core) * half_rows, half_rows)], their_half,
        pair_sems.at[0], pair_sems.at[1], partner,
    )

    @pl.when(jnp.logical_not(is_owner))
    def _():
        send(small_ref, small_recv.at[me], small_sems.at[0], small_sems.at[1], (0, 0))

    pair.wait()
    mine = grads_ref[pl.ds(pl.multiple_of(core * half_rows, half_rows), half_rows)]
    rs_src[...] = (mine + their_half[...]).astype(rs_src.dtype).reshape(rs_src.shape)

    def start_rs(step, carry):
        peer = chip_at(step, i, j)
        send(
            rs_src.at[peer[0] * 2 + peer[1] // 2], rs_recv.at[chip],
            rs_sems.at[0], rs_sems.at[1], peer,
        )
        return carry

    lax.fori_loop(1, chips, start_rs, 0)

    @pl.when(is_owner)
    def _():
        small_recv[0] = small_ref[...]
        await_bytes(small_recv.at[pl.ds(0, n - 1)], small_sems.at[1])
        small_sum[...] = jnp.sum(small_recv[...], axis=0)

        def start_small(step, carry):
            peer = peer_at(step, i, j)
            send(
                small_sum, small_total_ref, small_back_sems.at[0], small_back_sems.at[1], peer
            )
            return carry

        lax.fori_loop(1, n, start_small, 0)
        mine = pltpu.make_async_copy(small_sum, small_total_ref, local_sems.at[2])
        mine.start()
        mine.wait()
        await_bytes(small_recv.at[pl.ds(0, n - 1)], small_back_sems.at[0])

    @pl.when(jnp.logical_not(is_owner))
    def _():
        await_bytes(small_ref, small_sems.at[0])

    rs_recv[chip] = rs_src[chip]
    await_bytes(rs_src.at[pl.ds(0, chips - 1)], rs_sems.at[1])
    ag_src[...] = jnp.sum(rs_recv[...].astype(jnp.float32), axis=0).astype(ag_src.dtype)

    def start_ag(step, carry):
        peer = chip_at(step, i, j)
        send(ag_src, total_ref.at[core, chip], ag_sems.at[0], ag_sems.at[1], peer)
        return carry

    lax.fori_loop(1, chips, start_ag, 0)
    mine = pltpu.make_async_copy(ag_src, total_ref.at[core, chip], local_sems.at[3])
    mine.start()
    mine.wait()
    await_bytes(rs_src.at[pl.ds(0, chips - 1)], rs_sems.at[0])
    await_bytes(rs_src.at[pl.ds(0, chips - 1)], ag_sems.at[1])
    swap = send(
        total_ref.at[core], total_ref.at[core], swap_sems.at[0], swap_sems.at[1], partner
    )
    await_bytes(rs_src.at[pl.ds(0, chips - 1)], ag_sems.at[0])
    await_bytes(landed_ref.at[:, :, 0], local_sems.at[1])
    many = landed_ref.at[:, :, pl.ds(0, n - 1)]
    await_bytes(many, back_sems.at[0])
    await_bytes(many, back_sems.at[1])
    await_bytes(four_ref.at[:, :, :, pl.ds(0, n - 1)], out_sems.at[0])

    @pl.when(jnp.logical_not(is_owner))
    def _():
        await_bytes(small_ref, small_back_sems.at[1])

    swap.wait()


def whole_step_call(four, table, gain, w_in, b_in, w_mid, b_mid, w_out, n_lat, n_lev):
    members, kinds, slots, n, two, lanes = four.shape
    bf16, f32 = jnp.bfloat16, jnp.float32
    waves, longitudes = table.shape
    params = (table, table.T, gain[None], w_in, b_in[None], w_mid, b_mid[None], w_out)
    chips = n // 2
    grad_rows = (w_in.size + w_mid.size + w_out.size) // lanes
    half = grad_rows // 2
    slices = (chips, half // chips, lanes)
    small = (16, lanes)
    dma = pltpu.SemaphoreType.DMA
    return pl.pallas_call(
        functools.partial(whole_step, n),
        out_shape=(
            jax.ShapeDtypeStruct((members, slots, n, two, lanes), bf16),
            jax.ShapeDtypeStruct((2,) + slices, bf16),
            jax.ShapeDtypeStruct(small, f32),
        ),
        in_specs=[pl.BlockSpec(memory_space=pl.ANY)]
        + [pl.BlockSpec(memory_space=pltpu.VMEM)] * len(params),
        out_specs=[pl.BlockSpec(memory_space=pl.ANY)] * 3,
        scratch_shapes=[
            pltpu.VMEM((members, kinds, n_lev, n_lat * slots, two, lanes), bf16),
            pltpu.VMEM((members, n_lev, n_lat * slots, two, lanes), bf16),
            pltpu.VMEM((2 * longitudes, 2 * waves), bf16),
            pltpu.VMEM((2 * waves, 2 * longitudes), bf16),
            pltpu.VMEM((grad_rows, lanes), f32),
            pltpu.VMEM(small, f32),
            pltpu.VMEM((half, lanes), f32),
            pltpu.VMEM(slices, bf16),
            pltpu.VMEM(slices, bf16),
            pltpu.VMEM(slices[1:], bf16),
            pltpu.VMEM((n,) + small, f32),
            pltpu.VMEM(small, f32),
            dma((1,)),
            dma((members,)),
            dma((members,)),
        ]
        + [dma((2,))] * 7
        + [dma((4,))],
        compiler_params=pltpu.CompilerParams(
            has_side_effects=True, vmem_limit_bytes=60 * 1024 * 1024
        ),
        name="whole_step",
    )(four, *params)


def local(
    n_lat, n_lev, spec_in, cotangent, legendre, quad_weights, wave_order, norm_gain, weight_in,
    bias_in, weight_mid, bias_mid, weight_out,
):
    bf16 = jnp.bfloat16
    n = n_lat * n_lev
    slots_here, degrees, members, lanes = spec_in.shape
    rows = NLAT // n
    own_waves = lax.dynamic_slice_in_dim(wave_order, lax.axis_index("lat") * slots_here, slots_here)
    living, shrink = spectral_masks(own_waves, degrees)
    basis_rows = jnp.where(living[:, :, None], legendre, jnp.zeros_like(legendre))
    table = fourier_tables(wave_order)
    lane = np.arange(lanes)
    apart = np.zeros((lanes, lanes), np.float32)
    apart[lane, (lane % 2) * (lanes // 2) + lane // 2] = 1.0
    apart = jnp.asarray(apart, bf16)

    pushed = (time_step * cotangent.astype(jnp.float32) * shrink[:, :, None, None]).astype(bf16)
    both = jnp.stack([spec_in, pushed], axis=3)
    both = jnp.einsum("slehk,kq->slehq", both, apart, preferred_element_type=jnp.float32)
    fourier = jnp.einsum(
        "slt,slehq->sehtq", basis_rows, both.astype(bf16), preferred_element_type=jnp.float32
    )
    weights = jnp.stack([jnp.ones_like(quad_weights), quad_weights])
    fourier = (fourier * weights[None, None, :, :, None]).astype(bf16)
    fourier = fourier.transpose(1, 2, 0, 3, 4)
    fourier = fourier.reshape(members, 2, slots_here, n, rows, lanes)
    landed, total, small = whole_step_call(
        fourier, table, norm_gain, weight_in, bias_in, weight_mid, bias_mid, weight_out,
        n_lat, n_lev,
    )
    landed = landed.reshape(members, slots_here, n * rows, lanes)
    landed = jnp.einsum(
        "estq,kq->setk", landed, apart, preferred_element_type=jnp.float32
    ).astype(bf16)
    grad_spec = cotangent.astype(jnp.float32) * shrink[:, :, None, None] + jnp.einsum(
        "slt,setk->slek", basis_rows, landed, preferred_element_type=jnp.float32
    )
    factor = float(MEMBERS * NLAT * NLON) ** (-0.5)
    total = total.reshape(-1, lanes)
    out, at = [], 0
    for like in (weight_in, weight_mid, weight_out):
        size = like.size // lanes
        blocks = total[at : at + size].reshape(-1, like.shape[0], lanes)
        out.append(blocks.transpose(1, 0, 2).reshape(like.shape).astype(jnp.float32) * factor)
        at += size
    small = small.reshape(-1) * factor
    gain_end, in_end = norm_gain.size, norm_gain.size + bias_in.size
    return (
        grad_spec, small[:gain_end], out[0], small[gain_end:in_end], out[1],
        small[in_end : in_end + bias_mid.size], out[2],
    )


def solution(mesh):
    split = P("lat", None, None, "lev")
    placed = (split, split, P("lat", None, None)) + (P(),) * 8
    return jax.shard_map(
        functools.partial(local, mesh.shape["lat"], mesh.shape["lev"]),
        mesh=mesh,
        in_specs=placed,
        out_specs=(split,) + (P(),) * 6,
        check_vma=False,
    )
```

time: 154 us -> 140 us (0.909)
  Pallas kernels: 126 us -> 113 us
  other arithmetic: 8.57 us -> 6.97 us
    pallas_call x3 -> x1, Pallas kernels: 126 us -> 113 us  [whole_step_call(): pl.pallas_call(functools.partial(whole_step, n), out_shape=(jax.ShapeDtyp...]
    another operation x1 -> x2, other arithmetic: 2.96 us -> 4.75 us  [the longest x1 2.51 us: local(): both = jnp.stack([spec_in, pushed], axis=3)]
    unnamed x17 -> x21, local copies, waits for them, and re-layouts: 6 us -> 6 us
where the time goes in v3:
time: 140 us; the launch traced here: 139 us
  Pallas kernels  113 us (81%)
  local copies, waits for them, and re-layouts  12.3 us (9%)
  other arithmetic  6.97 us (5%)
  matrix products  6.23 us (4%)
    pallas_call x1, Pallas kernels, whole_step_call(): pl.pallas_call(functools.partial(whole_step, n), out_shape=(jax.ShapeDtyp...  113 us
    unnamed x21, local copies, waits for them, and re-layouts  6 us
    dot_general x1, matrix products, local(): jnp.einsum('slt,slehq->sehtq', basis_rows, both.astype(bf16), preferred_e...  3.52 us
    convert_element_type x1, local copies, waits for them, and re-layouts, local(): fourier = (fourier * weights[None, None, :, :, None]).astype(bf16)  2.81 us

profile of v3, /device:TPU:1, one launch (start us, length us, event | category | flops | bytes accessed | tf_op | source)
XLA Modules:
  0.0 139.2 jit_solution(16893229242264400213)
XLA Ops:
  0.6 0.8 broadcast_compare_fusion
  1.5 0.1 broadcast_select_fusion.3
  1.6 2.5 %fusion.16 = bf16[6,171,4,1,128]{4,1,2,0,3:T(8,128)(2,1)} fusion(f32[6,171]{1,0:T(8,128)S(1)} %get-tuple-element.27, bf16[6,171,4,128]{3,2,1,0:T(4,128)(2,1)} %param.13), kind=kLoop, calls=%fused_computation.13 | loop fusion | flops 1575936 | bytes 2105352 | tf_op jit(solution)/shard_map/stack | solution.py:388
  4.1 0.1 fusion.27
  4.2 1.1 copy.53
  5.3 3.5 %fusion = bf16[4,2,6,256,128]{3,4,1,0,2:T(8,128)(2,1)S(1)} fusion(f32[2,256]{1,0:T(2,128)S(1)} %stack.19, bf16[128,128,1,1,1]{1,0,4,3,2:T(8,128)(2,1)S(1)} %copy-done.7, bf16[6,171,256]{2,1,0:T(8,128)(2,1)} %param.14, pred[6,171]{1,0:T(8,128)(4,1)S(1)} %fusion.27, bf16[6,171,4,1,128]{4,1,2,0,3:T(8,128)(2,1)} %fusion.16, bf16[6,171,4,1,128]{4,1,2,0,3:T(8,128)(2,1)} %bitcast.66), kind=kOutput, calls=%fused_computation.1 | convolution fusion | flops 812388864 | bytes 5808130 | tf_op jit(solution)/shard_map/slt,slehq->sehtq/dot_general | solution.py:390
  8.9 2.8 %copy.21 = bf16[4,2,6,256,128]{4,3,2,1,0:T(8,128)(2,1)} copy(bf16[4,2,6,256,128]{3,4,1,0,2:T(8,128)(2,1)S(1)} %fusion) | data formatting | bytes 6291456 | tf_op jit(solution)/shard_map/convert_element_type | solution.py:394
  11.7 2.2 %multiply_convert_fusion.2 = (bf16[192,512]{0,1:T(8,128)(2,1)S(1)}, bf16[192,512]{0,1:T(8,128)(2,1)S(1)}) fusion(f32[192]{0:T(256)S(1)} %compare_select_fusion, s32[192]{0:T(256)S(1)} %copy-done.4), kind=kLoop, calls=%fused_computation.31 | loop fusion | flops 1867776 | bytes 394752 | tf_op jit(solution)/shard_map/convert
  13.9 0.1 pad_maximum_fusion.1
  14.1 0.9 copy.22.table_ref
  15.0 0.9 fusion.37.table_t_ref
  15.9 112.9 %whole_step.1 = (bf16[4,6,128,2,128]{4,3,2,1,0:T(2,128)(2,1)}, bf16[2,64,32,128]{3,2,1,0:T(8,128)(2,1)}, f32[16,128]{1,0:T(8,128)}) custom-call(bf16[4,2,6,128,2,128]{5,4,3,2,1,0:T(2,128)(2,1)} %bitcast.59, bf16[384,512]{1,0:T(8,128)(2,1)} %copy.22.table_ref, bf16[512,384]{1,0:T(8,128)(2,1)} %fusion.37.table_t_ref, f32[1,256]{1,0:T(1,128)} %bitcast.74, ...), custom_call_target="tpu_custom_call" | custom-call | tf_op jit(solution)/shard_map/whole_step/pallas_call | solution.py:334
  128.8 2.7 %fusion.1 = f32[6,171,4,128]{3,1,2,0:T(8,128)S(1)} fusion(bf16[128,128,1,1]{1,0,2,3:T(8,128)(2,1)S(1)} %copy-done.6, bf16[4,6,256,128]{3,2,1,0:T(8,128)(2,1)} %bitcast.76, f32[6,171]{1,0:T(8,128)S(1)} %get-tuple-element.26, bf16[6,171,4,128]{3,2,1,0:T(4,128)(2,1)S(1)} %copy-done.1, bf16[6,171,256]{2,1,0:T(8,128)(2,1)} %param.14, pred[6,171]{1,0:T(8,128)(4,1)S(1)} %fusion.27), kind=kOutput, calls=%fused_computation.4 | convolution fusion | flops 472911360 | bytes 5287946 | tf_op jit(solution)/shard_map/slt,setk->slek/dot_general | solution.py:405
  131.6 2.1 %copy.26 = f32[6,171,4,128]{3,2,1,0:T(4,128)} copy(f32[6,171,4,128]{3,1,2,0:T(8,128)S(1)} %fusion.1) | data formatting | bytes 4202496
  133.7 0.1 convert_multiply_fusion.3
  133.8 0.4 copy.25
  134.2 0.8 copy.55
  135.1 0.3 copy.23
  135.4 0.8 copy.56
  136.2 0.6 slice_bitcast_fusion
  136.8 0.1 convert_multiply_fusion.2
  136.9 0.7 copy.24
  137.6 1.0 copy.54
  138.6 0.6 slice_bitcast_fusion.2
  (20 shorter events, 0.1 us)
Async XLA Ops:
  0.6 3.5 %copy-start = (bf16[6,171,4,128]{3,2,1,0:T(4,128)(2,1)S(1)}, bf16[6,171,4,128]{3,2,1,0:T(4,128)(2,1)}, u32[]{:S(2)}) copy-start(bf16[6,171,4,128]{3,2,1,0:T(4,128)(2,1)} %param.12) | copy-start | bytes 3151876
  1.6 3.7 %copy-start.5 = (f32[256]{0:T(256)S(1)}, f32[256]{0:T(256)}, u32[]{:S(2)}) copy-start(f32[256]{0:T(256)} %param.15) | copy-start | bytes 3076
  1.6 3.7 %copy-start.7 = (bf16[128,128,1,1,1]{1,0,4,3,2:T(8,128)(2,1)S(1)}, bf16[128,128,1,1,1]{1,0,4,3,2:T(8,128)(2,1)}, u32[]{:S(2)}) copy-start(bf16[128,128,1,1,1]{1,0,4,3,2:T(8,128)(2,1)} %constant.61) | copy-start | bytes 98308
  8.8 2.8 %copy-start.4 = (s32[192]{0:T(256)S(1)}, s32[192]{0:T(256)}, u32[]{:S(2)}) copy-start(s32[192]{0:T(256)} %param.16) | copy-start | bytes 2308
  15.9 112.9 %copy-start.1 = (bf16[6,171,4,128]{3,2,1,0:T(4,128)(2,1)S(1)}, bf16[6,171,4,128]{3,2,1,0:T(4,128)(2,1)}, u32[]{:S(2)}) copy-start(bf16[6,171,4,128]{3,2,1,0:T(4,128)(2,1)} %param.13) | copy-start | bytes 3151876
  15.9 112.9 %copy-start.6 = (bf16[128,128,1,1]{1,0,2,3:T(8,128)(2,1)S(1)}, bf16[128,128,1,1]{1,0,2,3:T(8,128)(2,1)}, u32[]{:S(2)}) copy-start(bf16[128,128,1,1]{1,0,2,3:T(8,128)(2,1)} %constant.62) | copy-start | bytes 98308
  131.6 2.1 %copy-start.2 = (bf16[2,64,32,128]{3,2,1,0:T(8,128)(2,1)S(1)}, bf16[2,64,32,128]{3,2,1,0:T(8,128)(2,1)}, u32[]{:S(2)}) copy-start(bf16[2,64,32,128]{3,2,1,0:T(8,128)(2,1)} %get-tuple-element.12) | copy-start | bytes 3145732
  133.8 2.4 %copy-start.3 = (f32[16,128]{1,0:T(8,128)S(1)}, f32[16,128]{1,0:T(8,128)}, u32[]{:S(2)}) copy-start(f32[16,128]{1,0:T(8,128)} %get-tuple-element.11) | copy-start | bytes 24580

commit v4 on v3

--- a/solution.py
+++ b/solution.py
@@ -28,38 +28,54 @@
     return (living, shrink)
 
 
-def fourier_tables(waves_all):
-    longitude = jnp.arange(NLON, dtype=jnp.int32)
-    phase_steps = waves_all[:, None] * longitude[None, :] % NLON
+def fourier_table(waves_all):
+    shape = (NLON, waves_all.shape[1])
+    longitude = lax.broadcasted_iota(jnp.int32, shape, 0)
+    phase_steps = jnp.bitwise_and(waves_all * longitude, NLON - 1)
     angles = phase_steps.astype(jnp.float32) * (2.0 * math.pi / NLON)
-    weight_scale = jnp.where(waves_all < WAVES, math.sqrt(2.0 / NLON), 0.0).astype(jnp.float32)[
-        :, None
-    ]
-    table = jnp.concatenate(
-        [jnp.cos(angles) * weight_scale, -jnp.sin(angles) * weight_scale], axis=0
+    scale = jnp.where(waves_all < WAVES, math.sqrt(2.0 / NLON), 0.0).astype(jnp.float32)
+    return jnp.concatenate(
+        [jnp.cos(angles) * scale, -jnp.sin(angles) * scale], axis=1
     ).astype(jnp.bfloat16)
-    return table
-
-
-def part(value, size, of):
-    return lax.rem(value // of, size)
-
-
-def peer_at(step, i, j):
-    away = lax.rem(step * 37, 128)
-    z = lax.rem(i // 8 + lax.rem(away, 4), 4)
-    y = lax.rem(part(i, 4, 2) + part(away, 4, 4), 4)
-    x = lax.rem(lax.rem(i, 2) * 2 + j // 2 + part(away, 4, 16), 4)
-    core = lax.rem(j + away // 64, 2)
-    return z * 8 + y * 2 + x // 2, lax.rem(x, 2) * 2 + core
-
-
-def chip_at(step, i, j):
-    away = lax.rem(step * 37, 64)
-    z = lax.rem(i // 8 + lax.rem(away, 4), 4)
-    y = lax.rem(part(i, 4, 2) + part(away, 4, 4), 4)
-    x = lax.rem(lax.rem(i, 2) * 2 + j // 2 + away // 16, 4)
-    return z * 8 + y * 2 + x // 2, lax.rem(x, 2) * 2 + lax.rem(j, 2)
+
+
+AROUND = (
+    (1, 2), (2, 1), (0, 3), (3, 0), (1, 1), (2, 3), (0, 1), (3, 2), (1, 0), (2, 2), (0, 2),
+    (3, 1), (2, 0), (1, 3), (3, 3),
+)
+
+
+def each_chip(i, j, visit):
+    z = [lax.rem(i // 8 + d, 4) * 8 for d in range(4)]
+    y = [lax.rem(lax.rem(i // 2, 4) + d, 4) * 2 for d in range(4)]
+    x = lax.rem(i, 2) * 2 + j // 2
+
+    def along_x(d):
+        to = lax.rem(x + d, 4)
+        return to // 2, lax.rem(to, 2) * 2
+
+    for d in (1, 2, 3):
+        high, low = along_x(d)
+        visit(z[0] + y[0] + high, low)
+
+    def turn(a, carry):
+        across = [along_x(a + d) for d in range(4)]
+        for at, (dz, dy) in enumerate(AROUND):
+            high, low = across[at % 4]
+            visit(z[dz] + y[dy] + high, low)
+        return carry
+
+    lax.fori_loop(0, 4, turn, 0)
+
+
+def each_peer(i, j, visit):
+    visit(i, j + 1 - 2 * lax.rem(j, 2))
+
+    def both(lat, low):
+        visit(lat, low)
+        visit(lat, low + 1)
+
+    each_chip(i, j, both)
 
 
 def send(src, dst, send_sem, recv_sem, peer):
@@ -141,7 +157,7 @@
 
 
 def whole_step(
-    n, four_ref, table_ref, table_t_ref, gain_ref, w_in_ref, b_in_ref, w_mid_ref, b_mid_ref,
+    n, four_ref, waves_ref, gain_ref, w_in_ref, b_in_ref, w_mid_ref, b_mid_ref,
     w_out_ref, landed_ref, total_ref, small_total_ref,
     recv_ref, back_ref, syn_ref, ana_ref, grads_ref, small_ref,
     their_half, rs_src, rs_recv, ag_src, small_recv, small_sum,
@@ -156,36 +172,33 @@
     partner = (i, j + 1 - 2 * core)
     members, slots = landed_ref.shape[:2]
     levels = recv_ref.shape[2]
-    waves, longitudes = table_ref.shape
+    waves, longitudes = 2 * waves_ref.shape[1], NLON
     is_owner = me == 0
 
     def arriving(e):
         return recv_ref.at[e, :, j, pl.ds(i * slots, slots)]
 
     def start_out(e):
-        def start(step, carry):
-            peer = peer_at(step, i, j)
+        def visit(lat, lev):
             send(
-                four_ref.at[e, :, :, peer[0] * 4 + peer[1]], arriving(e),
-                out_sems.at[0], arrive_sems.at[e], peer,
+                four_ref.at[e, :, :, lat * 4 + lev], arriving(e),
+                out_sems.at[0], arrive_sems.at[e], (lat, lev),
             )
-            return carry
 
         pltpu.make_async_copy(four_ref.at[e, :, :, me], arriving(e), own_sems.at[e]).start()
-        lax.fori_loop(1, n, start, 0)
+        each_peer(i, j, visit)
 
     start_out(0)
     start_out(1)
     grads_ref[...] = jnp.zeros_like(grads_ref)
     small_ref[...] = jnp.zeros_like(small_ref)
+    table = fourier_table(waves_ref[...])
     for r in range(2):
         span = pl.ds(r * longitudes, longitudes)
-        syn_ref[span] = dot(
-            table_t_ref[...], one_of_two((waves, 2 * waves), 1, r), NN
-        ).astype(jnp.bfloat16)
-        ana_ref[:, span] = dot(
-            one_of_two((2 * waves, waves), 0, r), table_ref[...], NN
-        ).astype(jnp.bfloat16)
+        syn_ref[span] = dot(table, one_of_two((waves, 2 * waves), 1, r), NN).astype(jnp.bfloat16)
+        ana_ref[:, span] = dot(one_of_two((2 * waves, waves), 0, r), table, NT).astype(
+            jnp.bfloat16
+        )
 
     recv_rows = recv_ref.reshape(members, 2, levels, 2 * n // 4 * slots, recv_ref.shape[-1])
     back_rows = back_ref.reshape(members, levels, 2 * n // 4 * slots, back_ref.shape[-1])
@@ -210,19 +223,17 @@
                 axis=1,
             )
 
-        def start_back(step, carry):
-            peer = peer_at(step, i, j)
+        def visit(lat, lev):
             send(
-                back_ref.at[e, peer[1], pl.ds(peer[0] * slots, slots)], landed_ref.at[e, :, me],
-                back_sems.at[0], back_sems.at[1], peer,
+                back_ref.at[e, lev, pl.ds(lat * slots, slots)], landed_ref.at[e, :, me],
+                back_sems.at[0], back_sems.at[1], (lat, lev),
             )
-            return carry
 
         pltpu.make_async_copy(
             back_ref.at[e, j, pl.ds(i * slots, slots)], landed_ref.at[e, :, me],
             local_sems.at[1],
         ).start()
-        lax.fori_loop(1, n, start_back, 0)
+        each_peer(i, j, visit)
 
         normed, delta_one, act_one, delta_two, act_two, column_cot, gain_sum = rest
         first, second = w_in_ref.size // 128, w_mid_ref.size // 128
@@ -255,15 +266,13 @@
     mine = grads_ref[pl.ds(pl.multiple_of(core * half_rows, half_rows), half_rows)]
     rs_src[...] = (mine + their_half[...]).astype(rs_src.dtype).reshape(rs_src.shape)
 
-    def start_rs(step, carry):
-        peer = chip_at(step, i, j)
+    def visit_rs(lat, low):
         send(
-            rs_src.at[peer[0] * 2 + peer[1] // 2], rs_recv.at[chip],
-            rs_sems.at[0], rs_sems.at[1], peer,
+            rs_src.at[lat * 2 + low // 2], rs_recv.at[chip],
+            rs_sems.at[0], rs_sems.at[1], (lat, low + core),
         )
-        return carry
-
-    lax.fori_loop(1, chips, start_rs, 0)
+
+    each_chip(i, j, visit_rs)
 
     @pl.when(is_owner)
     def _():
@@ -271,14 +280,13 @@
         await_bytes(small_recv.at[pl.ds(0, n - 1)], small_sems.at[1])
         small_sum[...] = jnp.sum(small_recv[...], axis=0)
 
-        def start_small(step, carry):
-            peer = peer_at(step, i, j)
+        def visit_small(lat, lev):
             send(
-                small_sum, small_total_ref, small_back_sems.at[0], small_back_sems.at[1], peer
+                small_sum, small_total_ref, small_back_sems.at[0], small_back_sems.at[1],
+                (lat, lev),
             )
-            return carry
-
-        lax.fori_loop(1, n, start_small, 0)
+
+        each_peer(i, j, visit_small)
         mine = pltpu.make_async_copy(small_sum, small_total_ref, local_sems.at[2])
         mine.start()
         mine.wait()
@@ -292,12 +300,12 @@
     await_bytes(rs_src.at[pl.ds(0, chips - 1)], rs_sems.at[1])
     ag_src[...] = jnp.sum(rs_recv[...].astype(jnp.float32), axis=0).astype(ag_src.dtype)
 
-    def start_ag(step, carry):
-        peer = chip_at(step, i, j)
-        send(ag_src, total_ref.at[core, chip], ag_sems.at[0], ag_sems.at[1], peer)
-        return carry
-
-    lax.fori_loop(1, chips, start_ag, 0)
+    def visit_ag(lat, low):
+        send(
+            ag_src, total_ref.at[core, chip], ag_sems.at[0], ag_sems.at[1], (lat, low + core)
+        )
+
+    each_chip(i, j, visit_ag)
     mine = pltpu.make_async_copy(ag_src, total_ref.at[core, chip], local_sems.at[3])
     mine.start()
     mine.wait()
@@ -320,11 +328,11 @@
     swap.wait()
 
 
-def whole_step_call(four, table, gain, w_in, b_in, w_mid, b_mid, w_out, n_lat, n_lev):
+def whole_step_call(four, waves_all, gain, w_in, b_in, w_mid, b_mid, w_out, n_lat, n_lev):
     members, kinds, slots, n, two, lanes = four.shape
     bf16, f32 = jnp.bfloat16, jnp.float32
-    waves, longitudes = table.shape
-    params = (table, table.T, gain[None], w_in, b_in[None], w_mid, b_mid[None], w_out)
+    waves, longitudes = 2 * waves_all.shape[0], NLON
+    params = (waves_all[None], gain[None], w_in, b_in[None], w_mid, b_mid[None], w_out)
     chips = n // 2
     grad_rows = (w_in.size + w_mid.size + w_out.size) // lanes
     half = grad_rows // 2
@@ -378,7 +386,6 @@
     own_waves = lax.dynamic_slice_in_dim(wave_order, lax.axis_index("lat") * slots_here, slots_here)
     living, shrink = spectral_masks(own_waves, degrees)
     basis_rows = jnp.where(living[:, :, None], legendre, jnp.zeros_like(legendre))
-    table = fourier_tables(wave_order)
     lane = np.arange(lanes)
     apart = np.zeros((lanes, lanes), np.float32)
     apart[lane, (lane % 2) * (lanes // 2) + lane // 2] = 1.0
@@ -395,7 +402,7 @@
     fourier = fourier.transpose(1, 2, 0, 3, 4)
     fourier = fourier.reshape(members, 2, slots_here, n, rows, lanes)
     landed, total, small = whole_step_call(
-        fourier, table, norm_gain, weight_in, bias_in, weight_mid, bias_mid, weight_out,
+        fourier, wave_order, norm_gain, weight_in, bias_in, weight_mid, bias_mid, weight_out,
         n_lat, n_lev,
     )
     landed = landed.reshape(members, slots_here, n * rows, lanes)

time: 140 us -> 127 us (0.907)
  the two profiles are of different devices: /device:TPU:1 before, /device:TPU:19 now
where the time goes in v4:
time: 127 us
  Pallas kernels  104 us (82%)
  local copies, waits for them, and re-layouts  12 us (9%)
  matrix products  6.23 us (5%)
  other arithmetic  4.36 us (3%)
    pallas_call x1, Pallas kernels, whole_step_call(): pl.pallas_call(functools.partial(whole_step, n), out_shape=(jax.ShapeDtyp...  104 us
    unnamed x15, local copies, waits for them, and re-layouts  5.97 us
    dot_general x1, matrix products, local(): jnp.einsum('slt,slehq->sehtq', basis_rows, both.astype(bf16), preferred_e...  3.51 us
    convert_element_type x1, local copies, waits for them, and re-layouts, local(): fourier = (fourier * weights[None, None, :, :, None]).astype(bf16)  2.8 us
    dot_general x1, matrix products, local(): jnp.einsum('slt,setk->slek', basis_rows, landed, preferred_element_type=j...  2.71 us

profile of v4, /device:TPU:19, one launch (start us, length us, event | category | flops | bytes accessed | tf_op | source)
XLA Modules:
  0.0 127.1 jit_solution(12053227033570946235)
XLA Ops:
  0.6 0.0 copy-start
  0.6 0.8 broadcast_compare_fusion
  1.5 0.1 fusion.21
  1.6 0.7 stack.19
  2.3 0.1 broadcast_select_fusion.3
  2.3 2.5 %fusion.16 = bf16[6,171,4,1,128]{4,1,2,0,3:T(8,128)(2,1)} fusion(f32[6,171]{1,0:T(8,128)S(1)} %get-tuple-element.27, bf16[6,171,4,128]{3,2,1,0:T(4,128)(2,1)} %param.13), kind=kLoop, calls=%fused_computation.13 | loop fusion | flops 1575936 | bytes 2105352 | tf_op jit(solution)/shard_map/stack | solution.py:395
  4.8 1.1 copy.52
  6.0 0.0 copy-done.4
  6.0 3.5 %fusion = bf16[4,2,6,256,128]{3,4,1,0,2:T(8,128)(2,1)S(1)} fusion(f32[2,256]{1,0:T(2,128)S(1)} %stack.19, bf16[128,128,1,1,1]{1,0,4,3,2:T(8,128)(2,1)S(1)} %copy-done.4, bf16[6,171,256]{2,1,0:T(8,128)(2,1)} %param.14, pred[6,171]{1,0:T(8,128)(4,1)S(1)} %fusion.21, bf16[6,171,4,1,128]{4,1,2,0,3:T(8,128)(2,1)} %fusion.16, bf16[6,171,4,1,128]{4,1,2,0,3:T(8,128)(2,1)} %bitcast.65), kind=kOutput, calls=%fused_computation.1 | convolution fusion | flops 812388864 | bytes 5808130 | tf_op jit(solution)/shard_map/slt,slehq->sehtq/dot_general | solution.py:397
  9.5 2.8 %copy.21 = bf16[4,2,6,256,128]{4,3,2,1,0:T(8,128)(2,1)} copy(bf16[4,2,6,256,128]{3,4,1,0,2:T(8,128)(2,1)S(1)} %fusion) | data formatting | bytes 6291456 | tf_op jit(solution)/shard_map/convert_element_type | solution.py:401
  12.3 103.8 %whole_step.1 = (bf16[4,6,128,2,128]{4,3,2,1,0:T(2,128)(2,1)}, bf16[2,64,32,128]{3,2,1,0:T(8,128)(2,1)}, f32[16,128]{1,0:T(8,128)}) custom-call(bf16[4,2,6,128,2,128]{5,4,3,2,1,0:T(2,128)(2,1)} %bitcast.58, s32[1,192]{1,0:T(1,128)} %bitcast.71, f32[1,256]{1,0:T(1,128)} %bitcast.74, bf16[256,512]{1,0:T(8,128)(2,1)} %w_in_ref.1, f32[1,512]{1,0:T(1,128)} %bitcast.72, ...), custom_call_target="tpu_custom_call" | custom-call | tf_op jit(solution)/shard_map/whole_step/pallas_call | solution.py:342
  116.0 0.7 broadcast_multiply_fusion
  116.7 0.6 slice_bitcast_fusion.2
  117.3 0.6 slice_bitcast_fusion
  117.9 2.7 %fusion.1 = f32[6,171,4,128]{3,1,2,0:T(8,128)S(1)} fusion(bf16[128,128,1,1]{1,0,2,3:T(8,128)(2,1)S(1)} %copy-done.3, bf16[4,6,256,128]{3,2,1,0:T(8,128)(2,1)} %bitcast.76, f32[6,171]{1,0:T(8,128)S(1)} %get-tuple-element.26, bf16[6,171,4,128]{3,2,1,0:T(4,128)(2,1)S(1)} %copy-done.1, bf16[6,171,256]{2,1,0:T(8,128)(2,1)} %param.14, pred[6,171]{1,0:T(8,128)(4,1)S(1)} %fusion.21), kind=kOutput, calls=%fused_computation.4 | convolution fusion | flops 472911360 | bytes 5287946 | tf_op jit(solution)/shard_map/slt,setk->slek/dot_general | solution.py:412
  120.6 2.1 %copy.25 = f32[6,171,4,128]{3,2,1,0:T(4,128)} copy(f32[6,171,4,128]{3,1,2,0:T(8,128)S(1)} %fusion.1) | data formatting | bytes 4202496
  122.8 0.1 convert_multiply_fusion.2
  122.9 0.7 copy.23
  123.5 1.0 copy.53
  124.6 0.1 convert_multiply_fusion.3
  124.7 0.4 copy.24
  125.1 0.8 copy.54
  125.9 0.3 copy.22
  126.2 0.8 copy.55
  (9 shorter events, 0.0 us)
Async XLA Ops:
  0.6 4.2 %copy-start = (bf16[6,171,4,128]{3,2,1,0:T(4,128)(2,1)S(1)}, bf16[6,171,4,128]{3,2,1,0:T(4,128)(2,1)}, u32[]{:S(2)}) copy-start(bf16[6,171,4,128]{3,2,1,0:T(4,128)(2,1)} %param.12) | copy-start | bytes 3151876
  2.3 3.6 %copy-start.4 = (bf16[128,128,1,1,1]{1,0,4,3,2:T(8,128)(2,1)S(1)}, bf16[128,128,1,1,1]{1,0,4,3,2:T(8,128)(2,1)}, u32[]{:S(2)}) copy-start(bf16[128,128,1,1,1]{1,0,4,3,2:T(8,128)(2,1)} %constant.41) | copy-start | bytes 98308
  12.3 105.6 %copy-start.1 = (bf16[6,171,4,128]{3,2,1,0:T(4,128)(2,1)S(1)}, bf16[6,171,4,128]{3,2,1,0:T(4,128)(2,1)}, u32[]{:S(2)}) copy-start(bf16[6,171,4,128]{3,2,1,0:T(4,128)(2,1)} %param.13) | copy-start | bytes 3151876
  12.3 105.6 %copy-start.3 = (bf16[128,128,1,1]{1,0,2,3:T(8,128)(2,1)S(1)}, bf16[128,128,1,1]{1,0,2,3:T(8,128)(2,1)}, u32[]{:S(2)}) copy-start(bf16[128,128,1,1]{1,0,2,3:T(8,128)(2,1)} %constant.42) | copy-start | bytes 98308
  120.6 2.1 %copy-start.2 = (bf16[2,64,32,128]{3,2,1,0:T(8,128)(2,1)S(1)}, bf16[2,64,32,128]{3,2,1,0:T(8,128)(2,1)}, u32[]{:S(2)}) copy-start(bf16[2,64,32,128]{3,2,1,0:T(8,128)(2,1)} %get-tuple-element.12) | copy-start | bytes 3145732

commit v5 on v4

--- a/solution.py
+++ b/solution.py
@@ -158,11 +158,11 @@
 
 def whole_step(
     n, four_ref, waves_ref, gain_ref, w_in_ref, b_in_ref, w_mid_ref, b_mid_ref,
-    w_out_ref, landed_ref, total_ref, small_total_ref,
+    w_out_ref, landed_ref, g_in_ref, g_mid_ref, g_out_ref, g_gain_ref, g_b_in_ref, g_b_mid_ref,
     recv_ref, back_ref, syn_ref, ana_ref, grads_ref, small_ref,
-    their_half, rs_src, rs_recv, ag_src, small_recv, small_sum,
-    out_sems, arrive_sems, own_sems, pair_sems, back_sems, rs_sems, ag_sems, swap_sems,
-    small_sems, small_back_sems, local_sems,
+    their_half, their_small, rs_src, rs_recv, ag_src, total_ref, small_src, small_recv,
+    small_total, out_sems, arrive_sems, own_sems, pair_sems, back_sems, rs_sems, ag_sems,
+    swap_sems, small_sems, small_pair_sems, small_swap_sems, local_sems,
 ):
     i, j = lax.axis_index("lat"), lax.axis_index("lev")
     me = i * 4 + j
@@ -173,7 +173,6 @@
     members, slots = landed_ref.shape[:2]
     levels = recv_ref.shape[2]
     waves, longitudes = 2 * waves_ref.shape[1], NLON
-    is_owner = me == 0
 
     def arriving(e):
         return recv_ref.at[e, :, j, pl.ds(i * slots, slots)]
@@ -199,6 +198,19 @@
         ana_ref[:, span] = dot(one_of_two((2 * waves, waves), 0, r), table, NT).astype(
             jnp.bfloat16
         )
+
+    def start_back(e):
+        def visit(lat, lev):
+            send(
+                back_ref.at[e, lev, pl.ds(lat * slots, slots)], landed_ref.at[e, :, me],
+                back_sems.at[0], back_sems.at[1], (lat, lev),
+            )
+
+        pltpu.make_async_copy(
+            back_ref.at[e, j, pl.ds(i * slots, slots)], landed_ref.at[e, :, me],
+            local_sems.at[0],
+        ).start()
+        each_peer(i, j, visit)
 
     recv_rows = recv_ref.reshape(members, 2, levels, 2 * n // 4 * slots, recv_ref.shape[-1])
     back_rows = back_ref.reshape(members, levels, 2 * n // 4 * slots, back_ref.shape[-1])
@@ -223,17 +235,9 @@
                 axis=1,
             )
 
-        def visit(lat, lev):
-            send(
-                back_ref.at[e, lev, pl.ds(lat * slots, slots)], landed_ref.at[e, :, me],
-                back_sems.at[0], back_sems.at[1], (lat, lev),
-            )
-
-        pltpu.make_async_copy(
-            back_ref.at[e, j, pl.ds(i * slots, slots)], landed_ref.at[e, :, me],
-            local_sems.at[1],
-        ).start()
-        each_peer(i, j, visit)
+        @pl.when(e < members - 1)
+        def _():
+            start_back(e)
 
         normed, delta_one, act_one, delta_two, act_two, column_cot, gain_sum = rest
         first, second = w_in_ref.size // 128, w_mid_ref.size // 128
@@ -252,53 +256,38 @@
 
     lax.fori_loop(0, members, member, 0)
 
-    half_rows = their_half.shape[0]
+    half_rows, few = their_half.shape[0], their_small.shape[0]
     pair = send(
         grads_ref.at[pl.ds((1 - core) * half_rows, half_rows)], their_half,
         pair_sems.at[0], pair_sems.at[1], partner,
     )
-
-    @pl.when(jnp.logical_not(is_owner))
-    def _():
-        send(small_ref, small_recv.at[me], small_sems.at[0], small_sems.at[1], (0, 0))
-
+    small_pair = send(
+        small_ref.at[pl.ds((1 - core) * few, few)], their_small,
+        small_pair_sems.at[0], small_pair_sems.at[1], partner,
+    )
     pair.wait()
+    small_pair.wait()
     mine = grads_ref[pl.ds(pl.multiple_of(core * half_rows, half_rows), half_rows)]
     rs_src[...] = (mine + their_half[...]).astype(rs_src.dtype).reshape(rs_src.shape)
+    mine = small_ref[pl.ds(pl.multiple_of(core * few, few), few)]
+    small_src[...] = (mine + their_small[...]).astype(small_src.dtype)
 
     def visit_rs(lat, low):
+        peer = (lat, low + core)
         send(
-            rs_src.at[lat * 2 + low // 2], rs_recv.at[chip],
-            rs_sems.at[0], rs_sems.at[1], (lat, low + core),
+            rs_src.at[lat * 2 + low // 2], rs_recv.at[chip], rs_sems.at[0], rs_sems.at[1], peer
         )
+        send(small_src, small_recv.at[chip], small_sems.at[0], small_sems.at[1], peer)
 
     each_chip(i, j, visit_rs)
-
-    @pl.when(is_owner)
-    def _():
-        small_recv[0] = small_ref[...]
-        await_bytes(small_recv.at[pl.ds(0, n - 1)], small_sems.at[1])
-        small_sum[...] = jnp.sum(small_recv[...], axis=0)
-
-        def visit_small(lat, lev):
-            send(
-                small_sum, small_total_ref, small_back_sems.at[0], small_back_sems.at[1],
-                (lat, lev),
-            )
-
-        each_peer(i, j, visit_small)
-        mine = pltpu.make_async_copy(small_sum, small_total_ref, local_sems.at[2])
-        mine.start()
-        mine.wait()
-        await_bytes(small_recv.at[pl.ds(0, n - 1)], small_back_sems.at[0])
-
-    @pl.when(jnp.logical_not(is_owner))
-    def _():
-        await_bytes(small_ref, small_sems.at[0])
+    start_back(members - 1)
 
     rs_recv[chip] = rs_src[chip]
+    small_recv[chip] = small_src[...]
     await_bytes(rs_src.at[pl.ds(0, chips - 1)], rs_sems.at[1])
-    ag_src[...] = jnp.sum(rs_recv[...].astype(jnp.float32), axis=0).astype(ag_src.dtype)
+    summed = jnp.sum(rs_recv[...].astype(jnp.float32), axis=0).astype(ag_src.dtype)
+    ag_src[...] = summed
+    total_ref[core, chip] = summed
 
     def visit_ag(lat, low):
         send(
@@ -306,26 +295,41 @@
         )
 
     each_chip(i, j, visit_ag)
-    mine = pltpu.make_async_copy(ag_src, total_ref.at[core, chip], local_sems.at[3])
-    mine.start()
-    mine.wait()
-    await_bytes(rs_src.at[pl.ds(0, chips - 1)], rs_sems.at[0])
+    await_bytes(small_recv.at[pl.ds(0, chips - 1)], small_sems.at[1])
+    small_total[core] = jnp.sum(small_recv[...].astype(jnp.float32), axis=0)
+    small_swap = send(
+        small_total.at[core], small_total.at[core],
+        small_swap_sems.at[0], small_swap_sems.at[1], partner,
+    )
     await_bytes(rs_src.at[pl.ds(0, chips - 1)], ag_sems.at[1])
     swap = send(
         total_ref.at[core], total_ref.at[core], swap_sems.at[0], swap_sems.at[1], partner
     )
-    await_bytes(rs_src.at[pl.ds(0, chips - 1)], ag_sems.at[0])
-    await_bytes(landed_ref.at[:, :, 0], local_sems.at[1])
+    many = rs_src.at[pl.ds(0, chips - 1)]
+    await_bytes(many, rs_sems.at[0])
+    await_bytes(many, ag_sems.at[0])
+    await_bytes(small_recv.at[pl.ds(0, chips - 1)], small_sems.at[0])
+    await_bytes(landed_ref.at[:, :, 0], local_sems.at[0])
     many = landed_ref.at[:, :, pl.ds(0, n - 1)]
     await_bytes(many, back_sems.at[0])
     await_bytes(many, back_sems.at[1])
     await_bytes(four_ref.at[:, :, :, pl.ds(0, n - 1)], out_sems.at[0])
-
-    @pl.when(jnp.logical_not(is_owner))
-    def _():
-        await_bytes(small_ref, small_back_sems.at[1])
-
+    small_swap.wait()
+    factor = float(MEMBERS * NLAT * NLON) ** (-0.5)
+    at = 0
+    for ref in (g_gain_ref, g_b_in_ref, g_b_mid_ref):
+        for b in range(ref.shape[1] // 128):
+            row = small_total[at // few, pl.ds(at % few, 1)]
+            ref[:, b * 128 : (b + 1) * 128] = row * factor
+            at += 1
     swap.wait()
+    at, each = 0, total_ref.shape[2]
+    for ref in (g_in_ref, g_mid_ref, g_out_ref):
+        rows = ref.shape[0]
+        for b in range(ref.shape[1] // 128):
+            part = total_ref[at // half_rows, pl.ds(at % half_rows // each, rows // each)]
+            ref[:, b * 128 : (b + 1) * 128] = part.reshape(rows, 128)
+            at += rows
 
 
 def whole_step_call(four, waves_all, gain, w_in, b_in, w_mid, b_mid, w_out, n_lat, n_lev):
@@ -337,18 +341,26 @@
     grad_rows = (w_in.size + w_mid.size + w_out.size) // lanes
     half = grad_rows // 2
     slices = (chips, half // chips, lanes)
-    small = (16, lanes)
+    few = 8
+    small = (2 * few, lanes)
     dma = pltpu.SemaphoreType.DMA
+    row = lambda a: jax.ShapeDtypeStruct((1, a.size), f32)
+    out_shape = (
+        jax.ShapeDtypeStruct((members, slots, n, two, lanes), bf16),
+        jax.ShapeDtypeStruct(w_in.shape, bf16),
+        jax.ShapeDtypeStruct(w_mid.shape, bf16),
+        jax.ShapeDtypeStruct(w_out.shape, bf16),
+        row(gain),
+        row(b_in),
+        row(b_mid),
+    )
     return pl.pallas_call(
         functools.partial(whole_step, n),
-        out_shape=(
-            jax.ShapeDtypeStruct((members, slots, n, two, lanes), bf16),
-            jax.ShapeDtypeStruct((2,) + slices, bf16),
-            jax.ShapeDtypeStruct(small, f32),
-        ),
+        out_shape=out_shape,
         in_specs=[pl.BlockSpec(memory_space=pl.ANY)]
         + [pl.BlockSpec(memory_space=pltpu.VMEM)] * len(params),
-        out_specs=[pl.BlockSpec(memory_space=pl.ANY)] * 3,
+        out_specs=[pl.BlockSpec(memory_space=pl.ANY)]
+        + [pl.BlockSpec(memory_space=pltpu.VMEM)] * (len(out_shape) - 1),
         scratch_shapes=[
             pltpu.VMEM((members, kinds, n_lev, n_lat * slots, two, lanes), bf16),
             pltpu.VMEM((members, n_lev, n_lat * slots, two, lanes), bf16),
@@ -357,17 +369,20 @@
             pltpu.VMEM((grad_rows, lanes), f32),
             pltpu.VMEM(small, f32),
             pltpu.VMEM((half, lanes), f32),
+            pltpu.VMEM((few, lanes), f32),
             pltpu.VMEM(slices, bf16),
             pltpu.VMEM(slices, bf16),
             pltpu.VMEM(slices[1:], bf16),
-            pltpu.VMEM((n,) + small, f32),
-            pltpu.VMEM(small, f32),
+            pltpu.VMEM((2,) + slices, bf16),
+            pltpu.VMEM((few, lanes), bf16),
+            pltpu.VMEM((chips, few, lanes), bf16),
+            pltpu.VMEM((2, few, lanes), f32),
             dma((1,)),
             dma((members,)),
             dma((members,)),
         ]
-        + [dma((2,))] * 7
-        + [dma((4,))],
+        + [dma((2,))] * 8
+        + [dma((1,))],
         compiler_params=pltpu.CompilerParams(
             has_side_effects=True, vmem_limit_bytes=60 * 1024 * 1024
         ),
@@ -401,7 +416,7 @@
     fourier = (fourier * weights[None, None, :, :, None]).astype(bf16)
     fourier = fourier.transpose(1, 2, 0, 3, 4)
     fourier = fourier.reshape(members, 2, slots_here, n, rows, lanes)
-    landed, total, small = whole_step_call(
+    landed, g_in, g_mid, g_out, g_gain, g_b_in, g_b_mid = whole_step_call(
         fourier, wave_order, norm_gain, weight_in, bias_in, weight_mid, bias_mid, weight_out,
         n_lat, n_lev,
     )
@@ -413,19 +428,8 @@
         "slt,setk->slek", basis_rows, landed, preferred_element_type=jnp.float32
     )
     factor = float(MEMBERS * NLAT * NLON) ** (-0.5)
-    total = total.reshape(-1, lanes)
-    out, at = [], 0
-    for like in (weight_in, weight_mid, weight_out):
-        size = like.size // lanes
-        blocks = total[at : at + size].reshape(-1, like.shape[0], lanes)
-        out.append(blocks.transpose(1, 0, 2).reshape(like.shape).astype(jnp.float32) * factor)
-        at += size
-    small = small.reshape(-1) * factor
-    gain_end, in_end = norm_gain.size, norm_gain.size + bias_in.size
-    return (
-        grad_spec, small[:gain_end], out[0], small[gain_end:in_end], out[1],
-        small[in_end : in_end + bias_mid.size], out[2],
-    )
+    g_in, g_mid, g_out = (g.astype(jnp.float32) * factor for g in (g_in, g_mid, g_out))
+    return (grad_spec, g_gain[0], g_in, g_b_in[0], g_mid, g_b_mid[0], g_out)
 
 
 def solution(mesh):

time: 127 us -> 116 us (0.913)
  the two profiles are of different devices: /device:TPU:19 before, /device:TPU:1 now
where the time goes in v5:
time: 116 us
  Pallas kernels  92 us (79%)
  local copies, waits for them, and re-layouts  8.53 us (7%)
  other arithmetic  8.2 us (7%)
  matrix products  6.23 us (5%)
    pallas_call x1, Pallas kernels, whole_step_call(): pl.pallas_call(functools.partial(whole_step, n), out_shape=out_shape, in_...  92 us
    unnamed x21, local copies, waits for them, and re-layouts  5.01 us
    mul x3, other arithmetic, local(): g.astype(jnp.float32) * factor  4.71 us
    dot_general x1, matrix products, local(): jnp.einsum('slt,slehq->sehtq', basis_rows, both.astype(bf16), preferred_e...  3.51 us
    convert_element_type x1, local copies, waits for them, and re-layouts, local(): fourier = (fourier * weights[None, None, :, :, None]).astype(bf16)  2.82 us
    dot_general x1, matrix products, local(): jnp.einsum('slt,setk->slek', basis_rows, landed, preferred_element_type=j...  2.72 us
    another operation x1, other arithmetic, local(): both = jnp.stack([spec_in, pushed], axis=3)  2.49 us

profile of v5, /device:TPU:1, one launch (start us, length us, event | category | flops | bytes accessed | tf_op | source)
XLA Modules:
  0.0 115.7 jit_solution(10410345134104052227)
XLA Ops:
  0.6 0.0 copy-start
  0.6 0.8 broadcast_compare_fusion
  1.5 0.1 fusion.21
  1.6 0.7 stack.19
  2.3 0.1 broadcast_select_fusion.3
  2.3 2.5 %fusion.16 = bf16[6,171,4,1,128]{4,1,2,0,3:T(8,128)(2,1)} fusion(f32[6,171]{1,0:T(8,128)S(1)} %get-tuple-element.31, bf16[6,171,4,128]{3,2,1,0:T(4,128)(2,1)} %param.13), kind=kLoop, calls=%fused_computation.13 | loop fusion | flops 1575936 | bytes 2105352 | tf_op jit(solution)/shard_map/stack | solution.py:410
  4.8 0.0 copy-done
  4.8 1.1 copy.43
  6.0 0.0 copy-done.7
  6.0 3.5 %fusion = bf16[4,2,6,256,128]{3,4,1,0,2:T(8,128)(2,1)S(1)} fusion(f32[2,256]{1,0:T(2,128)S(1)} %stack.19, bf16[128,128,1,1,1]{1,0,4,3,2:T(8,128)(2,1)S(1)} %copy-done.7, bf16[6,171,256]{2,1,0:T(8,128)(2,1)} %param.14, pred[6,171]{1,0:T(8,128)(4,1)S(1)} %fusion.21, bf16[6,171,4,1,128]{4,1,2,0,3:T(8,128)(2,1)} %fusion.16, bf16[6,171,4,1,128]{4,1,2,0,3:T(8,128)(2,1)} %bitcast.37), kind=kOutput, calls=%fused_computation.1 | convolution fusion | flops 812388864 | bytes 5808130 | tf_op jit(solution)/shard_map/slt,slehq->sehtq/dot_general | solution.py:412
  9.5 2.8 %copy.21 = bf16[4,2,6,256,128]{4,3,2,1,0:T(8,128)(2,1)} copy(bf16[4,2,6,256,128]{3,4,1,0,2:T(8,128)(2,1)S(1)} %fusion) | data formatting | bytes 6291456 | tf_op jit(solution)/shard_map/convert_element_type | solution.py:416
  12.3 92.0 %whole_step.1 = (bf16[4,6,128,2,128]{4,3,2,1,0:T(2,128)(2,1)}, bf16[256,512]{1,0:T(8,128)(2,1)}, bf16[512,512]{1,0:T(8,128)(2,1)}, bf16[512,256]{1,0:T(8,128)(2,...) custom-call(bf16[4,2,6,128,2,128]{5,4,3,2,1,0:T(2,128)(2,1)} %bitcast.36, s32[1,192]{1,0:T(1,128)} %bitcast.38, ...), custom_call_target="tpu_custom_call" | custom-call | tf_op jit(solution)/shard_map/whole_step/pallas_call | solution.py:357
  104.3 1.8 %convert_multiply_fusion.4 = f32[256,512]{1,0:T(8,128)} fusion(bf16[256,512]{1,0:T(8,128)(2,1)} %get-tuple-element.16), kind=kLoop, calls=%fused_computation.20 | loop fusion | flops 262144 | bytes 786432 | tf_op jit(solution)/shard_map/mul | solution.py:431
  106.1 1.8 %convert_multiply_fusion.3 = f32[512,256]{1,0:T(8,128)} fusion(bf16[512,256]{1,0:T(8,128)(2,1)} %get-tuple-element.20), kind=kLoop, calls=%fused_computation.19 | loop fusion | flops 262144 | bytes 786432 | tf_op jit(solution)/shard_map/mul | solution.py:431
  107.9 0.0 copy-done.1
  107.9 0.0 copy-done.6
  107.9 2.7 %fusion.1 = f32[6,171,4,128]{3,1,2,0:T(8,128)S(1)} fusion(bf16[128,128,1,1]{1,0,2,3:T(8,128)(2,1)S(1)} %copy-done.6, bf16[4,6,256,128]{3,2,1,0:T(8,128)(2,1)} %bitcast.46, f32[6,171]{1,0:T(8,128)S(1)} %get-tuple-element.30, bf16[6,171,4,128]{3,2,1,0:T(4,128)(2,1)S(1)} %copy-done.1, bf16[6,171,256]{2,1,0:T(8,128)(2,1)} %param.14, pred[6,171]{1,0:T(8,128)(4,1)S(1)} %fusion.21), kind=kOutput, calls=%fused_computation.4 | convolution fusion | flops 472911360 | bytes 5287946 | tf_op jit(solution)/shard_map/slt,setk->slek/dot_general | solution.py:427
  110.7 0.0 copy-start.2
  110.7 2.1 %copy.22 = f32[6,171,4,128]{3,2,1,0:T(4,128)} copy(f32[6,171,4,128]{3,1,2,0:T(8,128)S(1)} %fusion.1) | data formatting | bytes 4202496
  112.8 0.0 copy-done.2
  112.8 1.1 convert_multiply_fusion.2
  113.9 0.6 copy.47
  114.5 0.6 copy.48
  115.1 0.6 copy.49
  (10 shorter events, 0.0 us)
Async XLA Ops:
  0.6 4.2 %copy-start = (bf16[6,171,4,128]{3,2,1,0:T(4,128)(2,1)S(1)}, bf16[6,171,4,128]{3,2,1,0:T(4,128)(2,1)}, u32[]{:S(2)}) copy-start(bf16[6,171,4,128]{3,2,1,0:T(4,128)(2,1)} %param.12) | copy-start | bytes 3151876
  2.3 3.6 %copy-start.7 = (bf16[128,128,1,1,1]{1,0,4,3,2:T(8,128)(2,1)S(1)}, bf16[128,128,1,1,1]{1,0,4,3,2:T(8,128)(2,1)}, u32[]{:S(2)}) copy-start(bf16[128,128,1,1,1]{1,0,4,3,2:T(8,128)(2,1)} %constant.40) | copy-start | bytes 98308
  12.3 95.6 %copy-start.1 = (bf16[6,171,4,128]{3,2,1,0:T(4,128)(2,1)S(1)}, bf16[6,171,4,128]{3,2,1,0:T(4,128)(2,1)}, u32[]{:S(2)}) copy-start(bf16[6,171,4,128]{3,2,1,0:T(4,128)(2,1)} %param.13) | copy-start | bytes 3151876
  12.3 95.6 %copy-start.6 = (bf16[128,128,1,1]{1,0,2,3:T(8,128)(2,1)S(1)}, bf16[128,128,1,1]{1,0,2,3:T(8,128)(2,1)}, u32[]{:S(2)}) copy-start(bf16[128,128,1,1]{1,0,2,3:T(8,128)(2,1)} %constant.41) | copy-start | bytes 98308
  110.7 2.2 %copy-start.2 = (bf16[512,512]{1,0:T(8,128)(2,1)S(1)}, bf16[512,512]{1,0:T(8,128)(2,1)}, u32[]{:S(2)}) copy-start(bf16[512,512]{1,0:T(8,128)(2,1)} %get-tuple-element.18) | copy-start | bytes 1572868
  110.7 3.3 %copy-start.5 = (f32[1,256]{1,0:T(1,128)S(1)}, f32[1,256]{1,0:T(1,128)}, u32[]{:S(2)}) copy-start(f32[1,256]{1,0:T(1,128)} %get-tuple-element.15) | copy-start | bytes 3076
  110.7 3.8 %copy-start.4 = (f32[1,512]{1,0:T(1,128)S(1)}, f32[1,512]{1,0:T(1,128)}, u32[]{:S(2)}) copy-start(f32[1,512]{1,0:T(1,128)} %get-tuple-element.17) | copy-start | bytes 6148
  110.7 4.4 %copy-start.3 = (f32[1,512]{1,0:T(1,128)S(1)}, f32[1,512]{1,0:T(1,128)}, u32[]{:S(2)}) copy-start(f32[1,512]{1,0:T(1,128)} %get-tuple-element.19) | copy-start | bytes 6148

commit v6 on v5

--- a/solution.py
+++ b/solution.py
@@ -156,12 +156,60 @@
     return back, (normed, delta_one, act_one, delta_two, act_two, column_cot, gain_sum)
 
 
+def legendre_out(
+    first_slot, orders_ref, quad_ref, spec_ref, cotangent_ref, legendre_ref, four_ref
+):
+    bf16, f32 = jnp.bfloat16, jnp.float32
+    slots, degrees, members, lanes = spec_ref.shape
+    pad = -(-degrees // 16) * 16
+    rows = degrees * members
+    spec_rows = spec_ref.reshape(slots, rows, lanes)
+    cotangent_rows = cotangent_ref.reshape(slots, rows, lanes)
+    four_rows = four_ref.reshape(members, 2, slots, NLAT, lanes)
+    a = lax.broadcasted_iota(jnp.int32, (lanes, lanes), 0)
+    b = lax.broadcasted_iota(jnp.int32, (lanes, lanes), 1)
+    apart = jnp.where(
+        a == jnp.where(b < lanes // 2, 2 * b, 2 * b - lanes + 1), 1.0, 0.0
+    ).astype(bf16)
+    degree = lax.broadcasted_iota(jnp.int32, (pad, rows), 0)
+    row = lax.broadcasted_iota(jnp.int32, (pad, rows), 1)
+    pick = jnp.concatenate(
+        [jnp.where(row == members * degree + e, 1.0, 0.0).astype(bf16) for e in range(members)],
+        axis=0,
+    )
+    quad = jnp.broadcast_to(quad_ref[...], (lanes, NLAT)).T
+
+    def slot(s, carry):
+        order = orders_ref[first_slot + s]
+        degree = lax.shift_right_logical(lax.broadcasted_iota(jnp.int32, (rows, lanes), 0), 2)
+        ratio = (degree * (degree + 1)).astype(f32) / float(WAVES * (WAVES - 1))
+        living = jnp.logical_and(degree >= order, order < WAVES)
+        shrink = jnp.where(living, 1.0 / (1.0 + ratio * ratio), 0.0)
+        pushed = (time_step * cotangent_rows[s].astype(f32) * shrink).astype(bf16)
+        both = jnp.concatenate(
+            [dot(spec_rows[s], apart, NN).astype(bf16), dot(pushed, apart, NN).astype(bf16)],
+            axis=1,
+        )
+        both = dot(pick, both, NN).astype(bf16)
+        basis = legendre_ref[s].astype(f32)
+        degree = lax.broadcasted_iota(jnp.int32, basis.shape, 0)
+        living = jnp.logical_and(degree >= order, order < WAVES)
+        basis = jnp.where(living, basis, 0.0).astype(bf16)
+        for e in range(members):
+            values = dot(basis, both[e * pad : e * pad + degrees], TN)
+            four_rows[e, 0, s] = values[:, :lanes].astype(bf16)
+            four_rows[e, 1, s] = (values[:, lanes:] * quad).astype(bf16)
+        return carry
+
+    lax.fori_loop(0, slots, slot, 0)
+
+
 def whole_step(
-    n, four_ref, waves_ref, gain_ref, w_in_ref, b_in_ref, w_mid_ref, b_mid_ref,
+    n, orders_ref, quad_ref, spec_ref, cotangent_ref, legendre_ref, waves_ref, gain_ref, w_in_ref, b_in_ref, w_mid_ref, b_mid_ref,
     w_out_ref, landed_ref, g_in_ref, g_mid_ref, g_out_ref, g_gain_ref, g_b_in_ref, g_b_mid_ref,
-    recv_ref, back_ref, syn_ref, ana_ref, grads_ref, small_ref,
+    four_ref, recv_ref, back_ref, syn_ref, ana_ref, grads_ref, small_ref,
     their_half, their_small, rs_src, rs_recv, ag_src, total_ref, small_src, small_recv,
-    small_total, out_sems, arrive_sems, own_sems, pair_sems, back_sems, rs_sems, ag_sems,
+    small_total, out_sems, arrive_sems, pair_sems, back_sems, rs_sems, ag_sems,
     swap_sems, small_sems, small_pair_sems, small_swap_sems, local_sems,
 ):
     i, j = lax.axis_index("lat"), lax.axis_index("lev")
@@ -184,9 +232,17 @@
                 out_sems.at[0], arrive_sems.at[e], (lat, lev),
             )
 
-        pltpu.make_async_copy(four_ref.at[e, :, :, me], arriving(e), own_sems.at[e]).start()
         each_peer(i, j, visit)
-
+        recv_ref[e, :, j, pl.ds(i * slots, slots)] = four_ref[e, :, :, me]
+
+    barrier = pltpu.get_barrier_semaphore()
+
+    def greet(lat, lev):
+        pl.semaphore_signal(barrier, inc=1, device_id=(lat, lev), device_id_type=MESH)
+
+    each_peer(i, j, greet)
+    legendre_out(i * slots, orders_ref, quad_ref, spec_ref, cotangent_ref, legendre_ref, four_ref)
+    pl.semaphore_wait(barrier, n - 1)
     start_out(0)
     start_out(1)
     grads_ref[...] = jnp.zeros_like(grads_ref)
@@ -220,7 +276,6 @@
         def _():
             start_out(e + 2)
 
-        pltpu.make_async_copy(four_ref.at[e, :, :, me], arriving(e), own_sems.at[e]).wait()
         await_bytes(four_ref.at[e, :, :, pl.ds(0, n - 1)], arrive_sems.at[e])
         state = join_levels([recv_rows[e, 0, k] for k in range(levels)])
         cot = join_levels([recv_rows[e, 1, k] for k in range(levels)])
@@ -332,11 +387,12 @@
             at += rows
 
 
-def whole_step_call(four, waves_all, gain, w_in, b_in, w_mid, b_mid, w_out, n_lat, n_lev):
-    members, kinds, slots, n, two, lanes = four.shape
+def whole_step_call(spec_in, cotangent, legendre, quad, waves_all, gain, w_in, b_in, w_mid, b_mid, w_out, n_lat, n_lev):
+    slots, _, members, lanes = spec_in.shape
+    kinds, n, two = 2, n_lat * n_lev, NLAT // (n_lat * n_lev)
     bf16, f32 = jnp.bfloat16, jnp.float32
     waves, longitudes = 2 * waves_all.shape[0], NLON
-    params = (waves_all[None], gain[None], w_in, b_in[None], w_mid, b_mid[None], w_out)
+    params = (quad[None], spec_in, cotangent, legendre, waves_all[None], gain[None], w_in, b_in[None], w_mid, b_mid[None], w_out)
     chips = n // 2
     grad_rows = (w_in.size + w_mid.size + w_out.size) // lanes
     half = grad_rows // 2
@@ -357,11 +413,12 @@
     return pl.pallas_call(
         functools.partial(whole_step, n),
         out_shape=out_shape,
-        in_specs=[pl.BlockSpec(memory_space=pl.ANY)]
+        in_specs=[pl.BlockSpec(memory_space=pltpu.SMEM)]
         + [pl.BlockSpec(memory_space=pltpu.VMEM)] * len(params),
         out_specs=[pl.BlockSpec(memory_space=pl.ANY)]
         + [pl.BlockSpec(memory_space=pltpu.VMEM)] * (len(out_shape) - 1),
         scratch_shapes=[
+            pltpu.VMEM((members, kinds, slots, n, two, lanes), bf16),
             pltpu.VMEM((members, kinds, n_lev, n_lat * slots, two, lanes), bf16),
             pltpu.VMEM((members, n_lev, n_lat * slots, two, lanes), bf16),
             pltpu.VMEM((2 * longitudes, 2 * waves), bf16),
@@ -379,15 +436,14 @@
             pltpu.VMEM((2, few, lanes), f32),
             dma((1,)),
             dma((members,)),
-            dma((members,)),
         ]
         + [dma((2,))] * 8
         + [dma((1,))],
         compiler_params=pltpu.CompilerParams(
-            has_side_effects=True, vmem_limit_bytes=60 * 1024 * 1024
+            collective_id=0, has_side_effects=True, vmem_limit_bytes=60 * 1024 * 1024
         ),
         name="whole_step",
-    )(four, *params)
+    )(waves_all, *params)
 
 
 def local(
@@ -406,18 +462,8 @@
     apart[lane, (lane % 2) * (lanes // 2) + lane // 2] = 1.0
     apart = jnp.asarray(apart, bf16)
 
-    pushed = (time_step * cotangent.astype(jnp.float32) * shrink[:, :, None, None]).astype(bf16)
-    both = jnp.stack([spec_in, pushed], axis=3)
-    both = jnp.einsum("slehk,kq->slehq", both, apart, preferred_element_type=jnp.float32)
-    fourier = jnp.einsum(
-        "slt,slehq->sehtq", basis_rows, both.astype(bf16), preferred_element_type=jnp.float32
-    )
-    weights = jnp.stack([jnp.ones_like(quad_weights), quad_weights])
-    fourier = (fourier * weights[None, None, :, :, None]).astype(bf16)
-    fourier = fourier.transpose(1, 2, 0, 3, 4)
-    fourier = fourier.reshape(members, 2, slots_here, n, rows, lanes)
     landed, g_in, g_mid, g_out, g_gain, g_b_in, g_b_mid = whole_step_call(
-        fourier, wave_order, norm_gain, weight_in, bias_in, weight_mid, bias_mid, weight_out,
+        spec_in, cotangent, legendre, quad_weights, wave_order, norm_gain, weight_in, bias_in, weight_mid, bias_mid, weight_out,
         n_lat, n_lev,
     )
     landed = landed.reshape(members, slots_here, n * rows, lanes)

time: 116 us -> 104 us (0.90)
  local copies, waits for them, and re-layouts: 8.53 us -> 3.89 us
  other arithmetic: 8.2 us -> 3.73 us
  matrix products: 6.23 us -> 2.74 us
    dot_general x1 -> x0, matrix products: 3.51 us -> none  [local(): jnp.einsum('slt,slehq->sehtq', basis_rows, both.astype(bf16), preferred_e...]
    convert_element_type x1 -> x0, local copies, waits for them, and re-layouts: 2.82 us -> none  [local(): fourier = (fourier * weights[None, None, :, :, None]).astype(bf16)]
    another operation x1 -> x0, other arithmetic: 2.49 us -> none  [local(): both = jnp.stack([spec_in, pushed], axis=3)]
    mul x3, other arithmetic: 4.71 us -> 2.81 us  [local(): g.astype(jnp.float32) * factor]
    unnamed x21 -> x20, local copies, waits for them, and re-layouts: 5.01 us -> 3.89 us
where the time goes in v6:
time: 104 us
  Pallas kernels  92.9 us (89%)
  local copies, waits for them, and re-layouts  3.89 us (4%)
  other arithmetic  3.73 us (4%)
  matrix products  2.74 us (3%)
    pallas_call x1, Pallas kernels, whole_step_call(): pl.pallas_call(functools.partial(whole_step, n), out_shape=out_shape, in_...  92.9 us
    unnamed x20, local copies, waits for them, and re-layouts  3.89 us
    mul x3, other arithmetic, local(): g.astype(jnp.float32) * factor  2.81 us
    dot_general x1, matrix products, local(): jnp.einsum('slt,setk->slek', basis_rows, landed, preferred_element_type=j...  2.74 us

profile of v6, /device:TPU:1, one launch (start us, length us, event | category | flops | bytes accessed | tf_op | source)
XLA Modules:
  0.0 104.0 jit_solution(17201260614254718165)
XLA Ops:
  0.6 0.8 broadcast_compare_fusion
  1.4 0.1 broadcast_select_fusion
  1.5 0.1 fusion.10
  1.6 0.0 copy-start
  1.6 92.9 %whole_step.1 = (bf16[4,6,128,2,128]{4,3,2,1,0:T(2,128)(2,1)}, bf16[256,512]{1,0:T(8,128)(2,1)}, bf16[512,512]{1,0:T(8,128)(2,1)}, bf16[512,256]{1,0:T(8,128)(2,...) custom-call(s32[192]{0:T(256)} %orders_ref.1, f32[1,256]{1,0:T(1,128)} %bitcast.24, ...), custom_call_target="tpu_custom_call" | custom-call | tf_op jit(solution)/shard_map/whole_step/pallas_call | solution.py:413
  94.5 0.0 copy-done
  94.5 0.0 copy-done.7
  94.5 2.7 %multiply_add_fusion = f32[6,171,4,128]{3,1,2,0:T(8,128)S(1)} fusion(bf16[128,128,1,1]{1,0,2,3:T(8,128)(2,1)S(1)} %copy-done.7, bf16[4,6,256,128]{3,2,1,0:T(8,128)(2,1)} %bitcast.27, bf16[6,171,4,128]{3,2,1,0:T(4,128)(2,1)S(1)} %copy-done, f32[6,171]{1,0:T(8,128)S(1)} %broadcast_select_fusion, bf16[6,171,256]{2,1,0:T(8,128)(2,1)} %legendre_ref.1, ...), kind=kOutput, calls=%fused_computation | convolution fusion | flops 472911360 | bytes 5287946 | tf_op jit(solution)/shard_map/slt,setk->slek/dot_general | solution.py:473
  97.3 0.0 copy-start.1
  97.3 2.1 %copy.20 = f32[6,171,4,128]{3,2,1,0:T(4,128)} copy(f32[6,171,4,128]{3,1,2,0:T(8,128)S(1)} %multiply_add_fusion) | data formatting | bytes 4202496
  99.4 0.0 copy-done.1
  99.4 0.0 copy-start.5
  99.4 0.0 copy-start.4
  99.4 1.1 %convert_multiply_fusion = f32[512,512]{1,0:T(8,128)} fusion(bf16[512,512]{1,0:T(8,128)(2,1)S(1)} %copy-done.1), kind=kLoop, calls=%fused_computation.4 | loop fusion | flops 524288 | bytes 1572864 | tf_op jit(solution)/shard_map/mul | solution.py:477
  100.5 0.0 copy-done.3
  100.5 0.8 convert_multiply_fusion.1
  101.4 0.0 copy-done.2
  101.4 0.9 convert_multiply_fusion.2
  102.2 0.0 copy-done.6
  102.2 0.6 copy.33
  102.8 0.0 copy-done.5
  102.8 0.6 copy.34
  103.4 0.0 copy-done.4
  103.4 0.6 copy.35
  (5 shorter events, 0.0 us)
Async XLA Ops:
  1.6 92.9 %copy-start = (bf16[6,171,4,128]{3,2,1,0:T(4,128)(2,1)S(1)}, bf16[6,171,4,128]{3,2,1,0:T(4,128)(2,1)}, u32[]{:S(2)}) copy-start(bf16[6,171,4,128]{3,2,1,0:T(4,128)(2,1)} %cotangent_ref.1) | copy-start | bytes 3151876
  1.6 92.9 %copy-start.7 = (bf16[128,128,1,1]{1,0,2,3:T(8,128)(2,1)S(1)}, bf16[128,128,1,1]{1,0,2,3:T(8,128)(2,1)}, u32[]{:S(2)}) copy-start(bf16[128,128,1,1]{1,0,2,3:T(8,128)(2,1)} %constant.35) | copy-start | bytes 98308
  97.3 2.1 %copy-start.1 = (bf16[512,512]{1,0:T(8,128)(2,1)S(1)}, bf16[512,512]{1,0:T(8,128)(2,1)}, u32[]{:S(2)}) copy-start(bf16[512,512]{1,0:T(8,128)(2,1)} %get-tuple-element.18) | copy-start | bytes 1572868
  99.4 1.1 %copy-start.3 = (bf16[512,256]{1,0:T(8,128)(2,1)S(1)}, bf16[512,256]{1,0:T(8,128)(2,1)}, u32[]{:S(2)}) copy-start(bf16[512,256]{1,0:T(8,128)(2,1)} %get-tuple-element.20) | copy-start | bytes 786436
  99.4 2.0 %copy-start.2 = (bf16[256,512]{1,0:T(8,128)(2,1)S(1)}, bf16[256,512]{1,0:T(8,128)(2,1)}, u32[]{:S(2)}) copy-start(bf16[256,512]{1,0:T(8,128)(2,1)} %get-tuple-element.16) | copy-start | bytes 786436
  99.4 2.8 %copy-start.6 = (f32[1,256]{1,0:T(1,128)S(1)}, f32[1,256]{1,0:T(1,128)}, u32[]{:S(2)}) copy-start(f32[1,256]{1,0:T(1,128)} %get-tuple-element.15) | copy-start | bytes 3076
  99.4 3.4 %copy-start.5 = (f32[1,512]{1,0:T(1,128)S(1)}, f32[1,512]{1,0:T(1,128)}, u32[]{:S(2)}) copy-start(f32[1,512]{1,0:T(1,128)} %get-tuple-element.17) | copy-start | bytes 6148
  99.4 4.0 %copy-start.4 = (f32[1,512]{1,0:T(1,128)S(1)}, f32[1,512]{1,0:T(1,128)}, u32[]{:S(2)}) copy-start(f32[1,512]{1,0:T(1,128)} %get-tuple-element.19) | copy-start | bytes 6148

commit v7 on v6

--- a/solution.py
+++ b/solution.py
@@ -277,6 +277,12 @@
             start_out(e + 2)
 
         await_bytes(four_ref.at[e, :, :, pl.ds(0, n - 1)], arrive_sems.at[e])
+
+        @pl.when(e == members - 1)
+        def _():
+            for early in range(members - 1):
+                start_back(early)
+
         state = join_levels([recv_rows[e, 0, k] for k in range(levels)])
         cot = join_levels([recv_rows[e, 1, k] for k in range(levels)])
         back, rest = column_work(
@@ -289,10 +295,6 @@
                 [back[p * waves : (p + 1) * waves, k * half : (k + 1) * half] for p in range(2)],
                 axis=1,
             )
-
-        @pl.when(e < members - 1)
-        def _():
-            start_back(e)
 
         normed, delta_one, act_one, delta_two, act_two, column_cot, gain_sum = rest
         first, second = w_in_ref.size // 128, w_mid_ref.size // 128

time: 104 us -> 103 us (level)
  Pallas kernels: 92.9 us -> 91.6 us
    pallas_call x1, Pallas kernels: 92.9 us -> 91.6 us  [whole_step_call(): pl.pallas_call(functools.partial(whole_step, n), out_shape=out_shape, in_...]
where the time goes in v7:
time: 103 us
  Pallas kernels  91.6 us (89%)
  local copies, waits for them, and re-layouts  3.89 us (4%)
  other arithmetic  3.73 us (4%)
  matrix products  2.74 us (3%)
    pallas_call x1, Pallas kernels, whole_step_call(): pl.pallas_call(functools.partial(whole_step, n), out_shape=out_shape, in_...  91.6 us
    unnamed x20, local copies, waits for them, and re-layouts  3.89 us
    mul x3, other arithmetic, local(): g.astype(jnp.float32) * factor  2.81 us
    dot_general x1, matrix products, local(): jnp.einsum('slt,setk->slek', basis_rows, landed, preferred_element_type=j...  2.74 us

profile of v7, /device:TPU:1, one launch (start us, length us, event | category | flops | bytes accessed | tf_op | source)
XLA Modules:
  0.0 102.6 jit_solution(14339965340900991500)
XLA Ops:
  0.6 0.8 broadcast_compare_fusion
  1.4 0.1 broadcast_select_fusion
  1.5 0.1 fusion.10
  1.6 0.0 copy-start
  1.6 91.6 %whole_step.1 = (bf16[4,6,128,2,128]{4,3,2,1,0:T(2,128)(2,1)}, bf16[256,512]{1,0:T(8,128)(2,1)}, bf16[512,512]{1,0:T(8,128)(2,1)}, bf16[512,256]{1,0:T(8,128)(2,...) custom-call(s32[192]{0:T(256)} %orders_ref.1, f32[1,256]{1,0:T(1,128)} %bitcast.24, ...), custom_call_target="tpu_custom_call" | custom-call | tf_op jit(solution)/shard_map/whole_step/pallas_call | solution.py:415
  93.1 0.0 copy-done
  93.1 0.0 copy-done.7
  93.2 2.7 %multiply_add_fusion = f32[6,171,4,128]{3,1,2,0:T(8,128)S(1)} fusion(bf16[128,128,1,1]{1,0,2,3:T(8,128)(2,1)S(1)} %copy-done.7, bf16[4,6,256,128]{3,2,1,0:T(8,128)(2,1)} %bitcast.27, bf16[6,171,4,128]{3,2,1,0:T(4,128)(2,1)S(1)} %copy-done, f32[6,171]{1,0:T(8,128)S(1)} %broadcast_select_fusion, bf16[6,171,256]{2,1,0:T(8,128)(2,1)} %legendre_ref.1, ...), kind=kOutput, calls=%fused_computation | convolution fusion | flops 472911360 | bytes 5287946 | tf_op jit(solution)/shard_map/slt,setk->slek/dot_general | solution.py:475
  95.9 0.0 copy-start.1
  95.9 2.1 %copy.20 = f32[6,171,4,128]{3,2,1,0:T(4,128)} copy(f32[6,171,4,128]{3,1,2,0:T(8,128)S(1)} %multiply_add_fusion) | data formatting | bytes 4202496
  98.0 0.0 copy-done.1
  98.1 0.0 copy-start.5
  98.1 0.0 copy-start.4
  98.1 1.1 %convert_multiply_fusion = f32[512,512]{1,0:T(8,128)} fusion(bf16[512,512]{1,0:T(8,128)(2,1)S(1)} %copy-done.1), kind=kLoop, calls=%fused_computation.4 | loop fusion | flops 524288 | bytes 1572864 | tf_op jit(solution)/shard_map/mul | solution.py:479
  99.2 0.0 copy-done.3
  99.2 0.8 convert_multiply_fusion.1
  100.0 0.0 copy-done.2
  100.0 0.9 convert_multiply_fusion.2
  100.9 0.0 copy-done.6
  100.9 0.6 copy.33
  101.5 0.0 copy-done.5
  101.5 0.6 copy.34
  102.0 0.0 copy-done.4
  102.0 0.6 copy.35
  (5 shorter events, 0.0 us)
Async XLA Ops:
  1.6 91.6 %copy-start = (bf16[6,171,4,128]{3,2,1,0:T(4,128)(2,1)S(1)}, bf16[6,171,4,128]{3,2,1,0:T(4,128)(2,1)}, u32[]{:S(2)}) copy-start(bf16[6,171,4,128]{3,2,1,0:T(4,128)(2,1)} %cotangent_ref.1) | copy-start | bytes 3151876
  1.6 91.6 %copy-start.7 = (bf16[128,128,1,1]{1,0,2,3:T(8,128)(2,1)S(1)}, bf16[128,128,1,1]{1,0,2,3:T(8,128)(2,1)}, u32[]{:S(2)}) copy-start(bf16[128,128,1,1]{1,0,2,3:T(8,128)(2,1)} %constant.35) | copy-start | bytes 98308
  95.9 2.1 %copy-start.1 = (bf16[512,512]{1,0:T(8,128)(2,1)S(1)}, bf16[512,512]{1,0:T(8,128)(2,1)}, u32[]{:S(2)}) copy-start(bf16[512,512]{1,0:T(8,128)(2,1)} %get-tuple-element.18) | copy-start | bytes 1572868
  98.0 1.1 %copy-start.3 = (bf16[512,256]{1,0:T(8,128)(2,1)S(1)}, bf16[512,256]{1,0:T(8,128)(2,1)}, u32[]{:S(2)}) copy-start(bf16[512,256]{1,0:T(8,128)(2,1)} %get-tuple-element.20) | copy-start | bytes 786436
  98.0 2.0 %copy-start.2 = (bf16[256,512]{1,0:T(8,128)(2,1)S(1)}, bf16[256,512]{1,0:T(8,128)(2,1)}, u32[]{:S(2)}) copy-start(bf16[256,512]{1,0:T(8,128)(2,1)} %get-tuple-element.16) | copy-start | bytes 786436
  98.1 2.8 %copy-start.6 = (f32[1,256]{1,0:T(1,128)S(1)}, f32[1,256]{1,0:T(1,128)}, u32[]{:S(2)}) copy-start(f32[1,256]{1,0:T(1,128)} %get-tuple-element.15) | copy-start | bytes 3076
  98.1 3.4 %copy-start.5 = (f32[1,512]{1,0:T(1,128)S(1)}, f32[1,512]{1,0:T(1,128)}, u32[]{:S(2)}) copy-start(f32[1,512]{1,0:T(1,128)} %get-tuple-element.17) | copy-start | bytes 6148
  98.1 4.0 %copy-start.4 = (f32[1,512]{1,0:T(1,128)S(1)}, f32[1,512]{1,0:T(1,128)}, u32[]{:S(2)}) copy-start(f32[1,512]{1,0:T(1,128)} %get-tuple-element.19) | copy-start | bytes 6148
